TPU v7x, 128 devices: a whole 4x4x4 slice. The times are simulated.
128 devices in a mesh: row: 2 (over core), col: 4 (over x), depth: 16 (over z, y).
Axes of the slice: x: 4, y: 4, z: 4, core: 2. Of those that a mesh axis runs over, the one named last changes fastest.
Arguments:
- normed: bfloat16 [512, 16, 4608], P('col', 'depth', 'row'), may hold values from -6 to 6
- qkv_grad: bfloat16 [512, 16, 8192], P('row', 'depth', 'col'), may hold values from -0.09375 to 0.09375
- attn_out: bfloat16 [512, 16, 4096], P('col', 'depth', 'row'), may hold values from -6 to 6
- out_grad: bfloat16 [512, 16, 4608], P('row', 'depth', 'col'), may hold values from -0.09375 to 0.09375
Outputs:
- qkv_weight_grad: float32 [4608, 8192], P('row', ('col', 'depth'))
- o_weight_grad: float32 [4096, 4608], P('row', ('col', 'depth'))
All inputs are finite; a program needn't handle non-finite values.
Results may differ from a plain program's by a relative error of at most 0.0003.
Values may be sent and summed in bfloat16 or wider, within the bound.
A program may use at most 128 MiB of HBM per device.

v0:
```python
import jax
import jax.numpy as jnp
from jax import lax
from jax.sharding import PartitionSpec as P


def sent_to_all(x, axis):
    peers = lax.axis_size(axis)
    return lax.all_to_all(jnp.broadcast_to(x[None], (peers, *x.shape)), axis, 0, 0, tiled=True)


def in_order(tiles, dim):
    tiles = jnp.moveaxis(tiles, 0, dim)
    lengths = tiles.shape
    return tiles.reshape(*lengths[:dim], lengths[dim] * lengths[dim + 1], *lengths[dim + 2 :])


def gather_directly(x, axis, dim):
    tiles = sent_to_all(x, axis)
    return in_order(tiles, dim)


def outer_sum(left, right):
    return lax.dot_general(
        left, right, (((0,), (0,)), ((), ())), preferred_element_type=jnp.float32
    )


def flatten(block):
    return block.reshape(block.shape[0] * block.shape[1], block.shape[2])


def qkv_total(normed, qkv_grad):
    inputs = gather_directly(flatten(normed), "col", 0)
    partial_qkv = outer_sum(inputs, gather_directly(flatten(qkv_grad), "row", 0))
    return lax.psum_scatter(partial_qkv, "depth", scatter_dimension=1, tiled=True)


def out_total(attn_out, out_grad):
    attended = gather_directly(flatten(attn_out), "col", 0)
    partial_out = outer_sum(attended, gather_directly(flatten(out_grad), "row", 0))
    return lax.psum_scatter(partial_out, "depth", scatter_dimension=1, tiled=True)


def per_device(normed, qkv_grad, attn_out, out_grad):
    qkv_weight_grad = qkv_total(normed, qkv_grad)
    o_weight_grad = out_total(attn_out, out_grad)
    return (qkv_weight_grad, o_weight_grad)


def solution(mesh):
    in_specs = (
        P("col", "depth", "row"),
        P("row", "depth", "col"),
        P("col", "depth", "row"),
        P("row", "depth", "col"),
    )
    out_specs = (P("row", ("col", "depth")), P("row", ("col", "depth")))
    return jax.shard_map(
        per_device, mesh=mesh, in_specs=in_specs, out_specs=out_specs, check_vma=False
    )
```

profile of v0, /device:TPU:0, one launch (start us, length us, event | category | flops | bytes accessed | tf_op | source)
XLA Modules:
  0.0 269.6 jit_solution(8060894493169394907)
XLA Ops:
  7.2 0.0 copy-start.2
  7.2 0.0 reduce-scatter.7.cloned.1.call-start
  7.2 1.2 broadcast_in_dim.35
  8.4 4.7 %all_to_all.20 = bf16[2,256,1152]{2,1,0:T(8,128)(2,1)S(1)} all-to-all(bf16[2,256,1152]{2,1,0:T(8,128)(2,1)S(1)} %broadcast_in_dim.35), channel_id=1, replica_groups=mesh['row'=2,'col'=4,'depth'=16] {'row'}, dimensions={0} | all-to-all | bytes 2359296 | tf_op jit(solution)/shard_map/all_to_all | solution.py:9
  13.1 0.0 copy-done.2
  13.1 0.2 broadcast_in_dim.33
  13.4 30.8 %all_to_all.21 = bf16[4,128,2048]{2,1,0:T(8,128)(2,1)S(1)} all-to-all(bf16[4,128,2048]{2,1,0:T(8,128)(2,1)S(1)} %broadcast_in_dim.33), channel_id=1, replica_groups=mesh['row'=2,'col'=4,'depth'=16] {'col'}, dimensions={0} | all-to-all | bytes 4194304 | tf_op jit(solution)/shard_map/all_to_all | solution.py:9
  44.2 5.1 %fusion.1 = f32[2048,1152]{0,1:T(8,128)} fusion(bf16[512,2048]{1,0:T(8,128)(2,1)S(1)} %bitcast.15, bf16[512,1152]{1,0:T(8,128)(2,1)S(1)} %bitcast.16), kind=kOutput, calls=%fused_computation.1 | convolution fusion | flops 2415919104 | bytes 12713984 | tf_op jit(solution)/shard_map/dot_general | solution.py:24
  49.3 0.0 copy-start
  49.3 0.0 reduce-scatter.7.cloned.1.call-update
  49.4 0.0 reduce-scatter.5.cloned.1.call-start
  49.4 1.1 copy-done
  50.6 0.2 broadcast_in_dim.31
  50.8 0.0 copy-start.1
  50.8 5.5 %all_to_all.22 = bf16[2,256,2048]{2,1,0:T(8,128)(2,1)S(1)} all-to-all(bf16[2,256,2048]{2,1,0:T(8,128)(2,1)S(1)} %broadcast_in_dim.31), channel_id=1, replica_groups=mesh['row'=2,'col'=4,'depth'=16] {'row'}, dimensions={0} | all-to-all | bytes 4194304 | tf_op jit(solution)/shard_map/all_to_all | solution.py:9
  56.4 0.0 copy-done.1
  56.4 0.2 broadcast_in_dim.29
  56.5 32.2 %all_to_all.23 = bf16[4,128,2304]{2,1,0:T(8,128)(2,1)S(1)} all-to-all(bf16[4,128,2304]{2,1,0:T(8,128)(2,1)S(1)} %broadcast_in_dim.29), channel_id=1, replica_groups=mesh['row'=2,'col'=4,'depth'=16] {'col'}, dimensions={0} | all-to-all | bytes 4718592 | tf_op jit(solution)/shard_map/all_to_all | solution.py:9
  88.7 9.3 %fusion = f32[2304,2048]{1,0:T(8,128)} fusion(bf16[512,2304]{1,0:T(8,128)(2,1)S(1)} %bitcast.13, bf16[512,2048]{1,0:T(8,128)(2,1)S(1)} %bitcast.14), kind=kOutput, calls=%fused_computation | convolution fusion | flops 4831838208 | bytes 23330816 | tf_op jit(solution)/shard_map/dot_general | solution.py:24
  98.0 0.0 reduce-scatter.5.cloned.1.call-update
  98.0 40.2 %reduce-scatter.7.cloned.1.call-done = f32[2048,72]{0,1:T(8,128)} async-done(((f32[2048,1152]{0,1:T(8,128)}), f32[2048,72]{0,1:T(8,128)}) %reduce-scatter.7.cloned.1.call-update) | async-done | bytes 589840
  138.2 124.5 %reduce-scatter.5.cloned.1.call-done = f32[2304,128]{1,0:T(8,128)} async-done(((f32[2304,2048]{1,0:T(8,128)}), f32[2304,128]{1,0:T(8,128)}) %reduce-scatter.5.cloned.1.call-update) | async-done | bytes 1179664 | tf_op jit(solution)/shard_map/reduce_scatter | solution.py:36
Async XLA Ops:
  7.2 5.9 %copy-start.2 = (bf16[128,1,2048]{2,0,1:T(8,128)(2,1)S(1)}, bf16[128,1,2048]{2,0,1:T(8,128)(2,1)}, u32[]{:S(2)}) copy-start(bf16[128,1,2048]{2,0,1:T(8,128)(2,1)} %param.6) | copy-start | bytes 1572868
  7.2 131.0 %reduce-scatter.7.cloned.1.call-start = ((), (), s32[]{:S(2)}) async-start(), calls=%async_computation.7 | async-start | bytes 10027008
  49.3 1.2 copy-start
  49.4 213.4 %reduce-scatter.5.cloned.1.call-start = ((), (), s32[]{:S(2)}) async-start(), calls=%async_computation.6 | async-start | bytes 20054016 | tf_op jit(solution)/shard_map/reduce_scatter | solution.py:36
  50.8 5.6 %copy-start.1 = (bf16[128,1,2304]{2,0,1:T(8,128)(2,1)S(1)}, bf16[128,1,2304]{2,0,1:T(8,128)(2,1)}, u32[]{:S(2)}) copy-start(bf16[128,1,2304]{2,0,1:T(8,128)(2,1)} %param.4) | copy-start | bytes 1769476
Sparse Core Ops, SparseCore 0:
  49.5 88.6 reduce-scatter.6
  142.2 120.4 reduce-scatter.4
where the time goes:
time: 270 us
  waiting for transfers between devices  165 us (61%)
  blocking collectives  73.3 us (27%)
  matrix products  14.4 us (5%)
  between operations  14.1 us (5%)
  local copies, waits for them, and re-layouts  3 us (1%)
    reduce_scatter x1, waiting for transfers between devices, qkv_total(): lax.psum_scatter(partial_qkv, 'depth', scatter_dimension=1, tiled=True)  125 us
    all_to_all x4, blocking collectives, sent_to_all(): lax.all_to_all(jnp.broadcast_to(x[None], (peers, *x.shape)), axis, 0, 0,...  73.3 us
    unnamed x3, waiting for transfers between devices  40.2 us
    dot_general x2, matrix products, outer_sum(): lax.dot_general(left, right, (((0,), (0,)), ((), ())), preferred_element_...  14.4 us
  transfers between devices with their start and end apart: 2, of which 2 were waited for; matrix products, arithmetic and copies ran while one was open for 4% of the time, Pallas kernels for 0%

commit v1 on v0

v1 whole, which is shorter than its diff:
```python
import functools

import jax
import jax.numpy as jnp
from jax import lax
from jax.experimental import pallas as pl
from jax.experimental.pallas import tpu as pltpu
from jax.sharding import PartitionSpec as P

MESH = pl.DeviceIdType.MESH
F32 = jnp.float32
BF16 = jnp.bfloat16

STEP = {1: 1, 2: -1, 3: 2}
N_SEM = 160


def kernel(
    a_q, b_q, a_o, b_o, out_q, out_o,
    sa_q, va_q, at_q, vb_q, c_q, r1_q, r2_q, f_q,
    sa_o, va_o, vb_o, bt_o, c_o, r1_o, r2_o, f_o,
    ssem, rsem, lsem, qsem,
):
    row, x, depth = lax.axis_index("row"), lax.axis_index("col"), lax.axis_index("depth")
    z, y = depth // 4, depth % 4

    def at(dx=0, dy=0, dz=0):
        return (row, (x + dx + 4) % 4, ((z + dz + 4) % 4) * 4 + (y + dy + 4) % 4)

    def on(axis, step):
        return at(**{"d" + axis: step})

    sibling = (1 - row, x, depth)

    count = {"r": 0, "l": 0}
    sent, kept = [], []

    def send(src, dst, device):
        k = count["r"]
        count["r"] += 1
        copy = pltpu.make_async_remote_copy(
            src, dst, ssem.at[k], rsem.at[k], device_id=device, device_id_type=MESH
        )
        copy.start()
        sent.append(copy)
        return copy

    def local(src, dst):
        k = count["l"]
        count["l"] += 1
        copy = pltpu.make_async_copy(src, dst, lsem.at[k])
        copy.start()
        return copy

    w_q, w_o = 512, 512
    loads_sa_q, loads_sa_o = [], []
    for d in (1, 2, 3):
        to = (z + STEP[d] + 4) % 4
        main = pl.ds(pl.multiple_of(to * w_q, 128), w_q)
        rest = pl.ds(pl.multiple_of(4 * w_q + (to // 2) * 128, 128), 128)
        loads_sa_q.append((
            local(a_q.at[:, main], sa_q.at[d - 1, :, 0:w_q]),
            local(a_q.at[:, rest], sa_q.at[d - 1, :, w_q:w_q + 128]),
        ))
    main = pl.ds(pl.multiple_of(z * w_q, 128), w_q)
    rest = pl.ds(pl.multiple_of(4 * w_q + (z // 2) * 128, 128), 128)
    load_va_q = (
        local(a_q.at[:, main], va_q.at[0, x, :, 0:w_q]),
        local(a_q.at[:, rest], va_q.at[0, x, :, w_q:w_q + 128]),
    )
    mine = pl.ds(pl.multiple_of(row * 256, 256), 256)
    load_vb_q = local(b_q, vb_q.at[0, mine, :])
    for d in (1, 2, 3):
        to = (y + STEP[d] + 4) % 4
        loads_sa_o.append(local(a_o.at[:, pl.ds(pl.multiple_of(to * w_o, 128), w_o)], sa_o.at[d - 1]))
    load_va_o = local(a_o.at[:, pl.ds(pl.multiple_of(y * w_o, 128), w_o)], va_o.at[0, x])
    load_vb_o = local(b_o, vb_o.at[0, mine, :])

    barrier = pltpu.get_barrier_semaphore()
    peers = [sibling, at(dx=1), at(dx=-1)]
    for axis in "yz":
        peers += [on(axis, 1), on(axis, -1), on(axis, 2)]
    for peer in peers:
        pl.semaphore_signal(barrier, inc=1, device_id=peer, device_id_type=MESH)
    pl.semaphore_wait(barrier, len(peers))

    ex_q, ex_o = {}, {}
    for d in (1, 2, 3):
        for copy in loads_sa_q[d - 1]:
            copy.wait()
        ex_q[d] = send(sa_q.at[d - 1], va_q.at[d, x], on("z", STEP[d]))
    for copy in load_va_q:
        copy.wait()
    gx_q, gx_o = {}, {}

    def spread(va, gx, s):
        gx[s, 1] = send(va.at[s, x], va.at[s, x], at(dx=1))
        gx[s, -1] = send(va.at[s, x], va.at[s, x], at(dx=-1))

    def pass_on(va, gx, s):
        step = 1 if s < 2 else -1
        gx[s, step].wait_recv()
        came = (x - step + 4) % 4
        gx[s, 2] = send(va.at[s, came], va.at[s, came], at(dx=step))

    def rest_of(gx, s):
        gx[s, -1 if s < 2 else 1].wait_recv()

    spread(va_q, gx_q, 0)
    for d in (1, 2, 3):
        loads_sa_o[d - 1].wait()
        ex_o[d] = send(sa_o.at[d - 1], va_o.at[d, x], on("y", STEP[d]))

    def b_direct(vb, axis, cols):
        src = vb.at[0, mine, cols]
        return (
            send(src, vb.at[1, mine, cols], on(axis, 1)),
            send(src, vb.at[2, mine, cols], on(axis, -1)),
        )

    halves = [pl.ds(pl.multiple_of(row * 256 + h * 128, 128), 128) for h in (0, 1)]

    def b_relay(vb, axis, cols, direct):
        across = []
        relay = []
        for d in (1, 2):
            direct[d - 1].wait_recv()
            part = vb.at[d, halves[d - 1], cols]
            relay.append(send(part, vb.at[3, halves[d - 1], cols], on(axis, STEP[d])))
            across.append(send(vb.at[d, mine, cols], vb.at[d, mine, cols], sibling))
        return relay, across

    def b_last(vb, cols, relay):
        across = []
        for d in (1, 2):
            relay[d - 1].wait_recv()
            part = vb.at[3, halves[d - 1], cols]
            across.append(send(part, part, sibling))
        return across

    cols_q = [slice(0, 1024), slice(1024, 2048)]
    all_o = slice(0, 1152)
    load_vb_q.wait()
    bd_q = [b_direct(vb_q, "z", cols_q[0])]
    own_q = send(vb_q.at[0, mine, :], vb_q.at[0, mine, :], sibling)
    load_vb_o.wait()
    bd_o = b_direct(vb_o, "y", all_o)
    own_o = send(vb_o.at[0, mine, :], vb_o.at[0, mine, :], sibling)
    load_va_o.wait()

    even = z % 2 == 0

    def turn_q(s, c):
        piece = va_q[s, c]
        k = s * 512 + c * 128
        at_q[0:512, pl.ds(pl.multiple_of(k, 128), 128)] = piece[:, 0:512].T
        tail = piece[:, 512:640].T
        at_q[512:576, pl.ds(pl.multiple_of(k, 128), 128)] = jnp.where(even, tail[0:64], tail[64:128])

    for d in (1, 2):
        ex_q[d].wait_recv()
        spread(va_q, gx_q, d)
    pass_on(va_q, gx_q, 0)
    ex_q[3].wait_recv()
    spread(va_q, gx_q, 3)
    for s in (1, 2, 3):
        pass_on(va_q, gx_q, s)

    spread(va_o, gx_o, 0)
    for d in (1, 2, 3):
        ex_o[d].wait_recv()
        spread(va_o, gx_o, d)

    relay_q0, across_q0 = b_relay(vb_q, "z", cols_q[0], bd_q[0])
    bd_q.append(b_direct(vb_q, "z", cols_q[1]))
    relay_o, across_o = b_relay(vb_o, "y", all_o, bd_o)

    for s in range(4):
        rest_of(gx_q, s)
        gx_q[s, 2].wait_recv()

        @pl.loop(0, 4)
        def _(c):
            turn_q(s, c)

    across_q0 += b_last(vb_q, cols_q[0], relay_q0)
    own_q.wait_recv()
    for copy in across_q0:
        copy.wait_recv()

    def multiply_q(j):
        @pl.loop(0, 2)
        def _(n):
            cols = pl.ds(pl.multiple_of(j * 512 + n * 256, 256), 256)
            right = vb_q[:, :, cols].reshape(2048, 256)
            total = jnp.dot(at_q[...], right, preferred_element_type=F32)
            for c in (0, 1):
                for h in (0, 1):
                    c_q[j, 2 * n + c, h] = total[h * 288:(h + 1) * 288, c * 128:(c + 1) * 128]

    def multiply_o():
        @pl.loop(0, 4)
        def _(w):
            for h in (0, 1):
                right = va_o[:, :, :, h * 256:(h + 1) * 256].reshape(2048, 256)
                total = jnp.dot(bt_o[w], right, preferred_element_type=F32)
                for j in range(4):
                    c_o[w, j, h] = total[j * 72:(j + 1) * 72]

    def sum_1(part, w, r1, r2, axis):
        return {
            1: send(part((w + 2) % 4, 0), r1.at[0], on(axis, 1)),
            2: send(part((w + 2) % 4, 1), r1.at[1], on(axis, -1)),
            3: send(part((w + 1) % 4, 1), r2.at[0, 1], on(axis, 1)),
            4: send(part((w + 3) % 4, 0), r2.at[1, 0], on(axis, -1)),
        }

    def sum_2(part, w, r1, r2, axis, go):
        go[1].wait_recv()
        ref = part((w + 1) % 4, 0)
        ref[...] = ref[...] + r1[0]
        go[5] = send(ref, r2.at[0, 0], on(axis, 1))
        go[2].wait_recv()
        ref = part((w + 3) % 4, 1)
        ref[...] = ref[...] + r1[1]
        go[6] = send(ref, r2.at[1, 1], on(axis, -1))

    def sum_3(part, w, r2, go, put):
        go[3].wait_recv()
        go[6].wait_recv()
        put(1, part(w, 1)[...] + r2[0, 1] + r2[1, 1])
        go[4].wait_recv()
        go[5].wait_recv()
        put(0, part(w, 0)[...] + r2[0, 0] + r2[1, 0])

    flip = ((z + 1) // 2) % 2
    order_q = [1 - flip, flip, 2 + flip, 3 - flip]
    parts_q = [lambda w, h, j=j: c_q.at[j, w, h] for j in order_q]
    go_q, go_o = {}, {}

    def q1(s):
        multiply_q(order_q[s])
        go_q[s] = sum_1(parts_q[s], y, r1_q.at[s], r2_q.at[s], "y")

    def q2(s):
        sum_2(parts_q[s], y, r1_q.at[s], r2_q.at[s], "y", go_q[s])

    rows_main = pl.ds(pl.multiple_of(z * 512, 512), 512)
    rows_rest = pl.ds(pl.multiple_of(2048 + z * 64, 64), 64)

    def home_q(s):
        j = order_q[s]
        delta = (j - z + 4) % 4
        device = (row, x, j * 4 + y)
        pair = []
        for i, (lo, n, rows) in enumerate(((0, 512, rows_main), (512, 64, rows_rest))):
            pair.append((
                pltpu.make_async_remote_copy(
                    f_q.at[s, lo:lo + n], out_q.at[rows], qsem.at[0, s, i], qsem.at[1, delta, i],
                    device_id=device, device_id_type=MESH,
                ),
                pltpu.make_async_copy(f_q.at[s, lo:lo + n], out_q.at[rows], qsem.at[0, s, i]),
            ))
        return delta, pair

    def q3(s):
        def put(h, value):
            f_q[s, h * 288:(h + 1) * 288] = value

        sum_3(parts_q[s], y, r2_q.at[s], go_q[s], put)
        delta, pair = home_q(s)

        @pl.when(delta != 0)
        def _():
            for far, near in pair:
                far.start()

        @pl.when(delta == 0)
        def _():
            for far, near in pair:
                near.start()

    order_o = [(y + 1 + s) % 4 for s in range(4)]
    parts_o = [lambda w, h, j=j: c_o.at[w, j, h] for j in order_o]

    def o1(s):
        go_o[s] = sum_1(parts_o[s], z, r1_o.at[s], r2_o.at[s], "z")

    def o2(s):
        sum_2(parts_o[s], z, r1_o.at[s], r2_o.at[s], "z", go_o[s])

    lanes_o = pl.ds(pl.multiple_of(y * 512, 512), 512)
    home_o = {}

    def o3(s):
        def put(h, value):
            f_o[s, :, h * 256:(h + 1) * 256] = value

        sum_3(parts_o[s], z, r2_o.at[s], go_o[s], put)
        if s < 3:
            home_o[s] = send(f_o.at[s], out_o.at[:, lanes_o], (row, x, z * 4 + order_o[s]))
        else:
            home_o[s] = local(f_o.at[s], out_o.at[:, lanes_o])

    def turn_o(s, r):
        bt_o[:, :, s * 512 + r * 256:s * 512 + (r + 1) * 256] = vb_o[s, r * 256:(r + 1) * 256].T.reshape(4, 288, 256)

    q1(0)
    pass_on(va_o, gx_o, 0)
    pass_on(va_o, gx_o, 1)
    q1(1)
    pass_on(va_o, gx_o, 2)
    pass_on(va_o, gx_o, 3)
    across_o += b_last(vb_o, all_o, relay_o)
    q2(0)
    own_o.wait_recv()
    for copy in across_o:
        copy.wait_recv()
    turn_o(0, 0)
    turn_o(0, 1)
    q2(1)
    turn_o(1, 0)
    turn_o(1, 1)
    relay_q1, across_q1 = b_relay(vb_q, "z", cols_q[1], bd_q[1])
    q3(0)
    turn_o(2, 0)
    turn_o(2, 1)
    turn_o(3, 0)
    turn_o(3, 1)
    for s in range(4):
        rest_of(gx_o, s)
        gx_o[s, 2].wait_recv()
    multiply_o()
    o1(0)
    o1(1)
    across_q1 += b_last(vb_q, cols_q[1], relay_q1)
    for copy in across_q1:
        copy.wait_recv()
    q1(2)
    q3(1)
    q1(3)
    o2(0)
    o1(2)
    o2(1)
    o1(3)
    q2(2)
    o3(0)
    o3(1)
    o2(2)
    o2(3)
    q2(3)
    o3(2)
    o3(3)
    q3(2)
    q3(3)

    for s in range(3):
        home_o[s].wait_recv()
    home_o[3].wait()
    for s in range(4):
        delta, pair = home_q(s)

        @pl.when(delta != 0)
        def _():
            for far, near in pair:
                far.wait_send()

        @pl.when(delta == 0)
        def _():
            for far, near in pair:
                near.wait()

    for d in (1, 2, 3):
        for i, (lo, n) in enumerate(((0, 512), (512, 64))):
            pltpu.make_async_remote_copy(
                f_q.at[0, lo:lo + n], out_q.at[lo:lo + n], qsem.at[0, 0, i], qsem.at[1, d, i],
                device_id=on("z", -d), device_id_type=MESH,
            ).wait_recv()
    for copy in sent:
        copy.wait_send()
    assert count["r"] <= N_SEM and count["l"] <= 24, count


def per_device(normed, qkv_grad, attn_out, out_grad):
    flat = [v.reshape(v.shape[0] * v.shape[1], v.shape[2]) for v in (normed, qkv_grad, attn_out, out_grad)]
    hbm = pl.BlockSpec(memory_space=pl.ANY)
    out_q, out_o = pl.pallas_call(
        kernel,
        out_shape=(
            jax.ShapeDtypeStruct((2304, 128), F32),
            jax.ShapeDtypeStruct((72, 2048), F32),
        ),
        in_specs=[hbm] * 4,
        out_specs=[hbm] * 2,
        scratch_shapes=[
            pltpu.VMEM((3, 128, 640), BF16),
            pltpu.VMEM((4, 4, 128, 640), BF16),
            pltpu.VMEM((576, 2048), BF16),
            pltpu.VMEM((4, 512, 2048), BF16),
            pltpu.VMEM((4, 4, 2, 288, 128), F32),
            pltpu.VMEM((4, 2, 288, 128), F32),
            pltpu.VMEM((4, 2, 2, 288, 128), F32),
            pltpu.VMEM((4, 576, 128), F32),
            pltpu.VMEM((3, 128, 512), BF16),
            pltpu.VMEM((4, 4, 128, 512), BF16),
            pltpu.VMEM((4, 512, 1152), BF16),
            pltpu.VMEM((4, 288, 2048), BF16),
            pltpu.VMEM((4, 4, 2, 72, 256), F32),
            pltpu.VMEM((4, 2, 72, 256), F32),
            pltpu.VMEM((4, 2, 2, 72, 256), F32),
            pltpu.VMEM((4, 72, 512), F32),
            pltpu.SemaphoreType.DMA((N_SEM,)),
            pltpu.SemaphoreType.DMA((N_SEM,)),
            pltpu.SemaphoreType.DMA((24,)),
            pltpu.SemaphoreType.DMA((2, 4, 2)),
        ],
        compiler_params=pltpu.CompilerParams(
            collective_id=0, has_side_effects=True, vmem_limit_bytes=60 * 1024 * 1024
        ),
        name="weight_grads",
    )(*flat)
    return out_q, out_o.T


def solution(mesh):
    in_specs = (
        P("col", "depth", "row"),
        P("row", "depth", "col"),
        P("col", "depth", "row"),
        P("row", "depth", "col"),
    )
    out_specs = (P("row", ("col", "depth")), P("row", ("col", "depth")))
    return jax.shard_map(
        per_device, mesh=mesh, in_specs=in_specs, out_specs=out_specs, check_vma=False
    )
```

time: 270 us -> 114 us (0.42)
  waiting for transfers between devices: 165 us -> 0 us
  Pallas kernels: 0 us -> 110 us
  blocking collectives: 73.3 us -> 0 us
  matrix products: 14.4 us -> 0 us
  between operations: 14.1 us -> 0.65 us
    reduce_scatter x1 -> x0, waiting for transfers between devices: 125 us -> none  [qkv_total(): lax.psum_scatter(partial_qkv, 'depth', scatter_dimension=1, tiled=True)]
    pallas_call x0 -> x1, Pallas kernels: none -> 110 us  [per_device(): pl.pallas_call(kernel, out_shape=(jax.ShapeDtypeStruct((2304, 128), F32),...]
    all_to_all x4 -> x0, blocking collectives: 73.3 us -> none  [sent_to_all(): lax.all_to_all(jnp.broadcast_to(x[None], (peers, *x.shape)), axis, 0, 0,...]
    unnamed x3 -> x0, waiting for transfers between devices: 40.2 us -> none
    dot_general x2 -> x0, matrix products: 14.4 us -> none  [outer_sum(): lax.dot_general(left, right, (((0,), (0,)), ((), ())), preferred_element_...]
  transfers between devices with their start and end apart: 2 -> 0, of which waited for: 2 -> 0; matrix products, arithmetic and copies ran while one was open for 4% -> 0% of each run, Pallas kernels for 0% -> 0%
where the time goes in v1:
time: 114 us; the launch traced here: 113 us
  Pallas kernels  110 us (96%)
  local copies, waits for them, and re-layouts  3.24 us (3%)
    pallas_call x1, Pallas kernels, per_device(): pl.pallas_call(kernel, out_shape=(jax.ShapeDtypeStruct((2304, 128), F32),...  110 us
    unnamed x4, local copies, waits for them, and re-layouts  3.24 us

profile of v1, /device:TPU:0, one launch (start us, length us, event | category | flops | bytes accessed | tf_op | source)
XLA Modules:
  0.0 113.4 jit_solution(10862582588452470031)
XLA Ops:
  0.6 109.5 %weight_grads.1 = (f32[2304,128]{1,0:T(8,128)}, f32[72,2048]{1,0:T(8,128)}) custom-call(bf16[128,2304]{1,0:T(8,128)(2,1)} %bitcast.7, bf16[256,2048]{1,0:T(8,128)(2,1)} %bitcast.5, bf16[128,2048]{1,0:T(8,128)(2,1)} %bitcast.9, bf16[256,1152]{1,0:T(8,128)(2,1)} %bitcast.8), custom_call_target="tpu_custom_call" | custom-call | tf_op jit(solution)/shard_map/weight_grads/pallas_call | solution.py:387
  110.1 0.0 copy-start
  110.1 2.4 %copy.8 = f32[2304,128]{1,0:T(8,128)} copy(f32[2304,128]{1,0:T(8,128)} %get-tuple-element.8) | data formatting | bytes 2359296
  112.6 0.0 copy-done
  112.6 0.8 copy.9
Async XLA Ops:
  110.1 2.4 %copy-start = (f32[72,2048]{1,0:T(8,128)S(1)}, f32[72,2048]{1,0:T(8,128)}, u32[]{:S(2)}) copy-start(f32[72,2048]{1,0:T(8,128)} %get-tuple-element.5) | copy-start | bytes 1769476

commit v2 on v0

v2 whole, which is shorter than its diff:
```python
import jax
import jax.numpy as jnp
from jax import lax
from jax.experimental import pallas as pl
from jax.experimental.pallas import tpu as pltpu
from jax.sharding import PartitionSpec as P

MESH = pl.DeviceIdType.MESH
F32 = jnp.float32
BF16 = jnp.bfloat16

(EXQ, EXO, GQ, GO, HQ, HO, OWNQ, OWNO, DQ, DO, RQ, RO, AQ, AO, PQ, PO, IQ, IO, LQ, LO, FQ, FO) = range(22)
STEP = {1: 1, 2: -1, 3: 2}
N_SEM = 180


def kernel(
    a_q, b_q, a_o, b_o, out_q, out_o,
    la_q, ta_q, at_q, vb_q, c_q, r1_q, r2_q, f_q,
    sa_o, va_o, lb_o, bt_o, c_o, r1_o, r2_o, f_o,
    ssem, rsem, lsem,
):
    row, x, depth = lax.axis_index("row"), lax.axis_index("col"), lax.axis_index("depth")
    z, y = depth // 4, depth % 4

    def at(dx=0, dy=0, dz=0):
        return (row, (x + dx + 4) % 4, ((z + dz + 4) % 4) * 4 + (y + dy + 4) % 4)

    def on(axis, step):
        return at(**{"d" + axis: step})

    sibling = (1 - row, x, depth)

    barrier = pltpu.get_barrier_semaphore()
    peers = [sibling, at(dx=1), at(dx=-1)]
    for axis in "yz":
        peers += [on(axis, 1), on(axis, -1), on(axis, 2)]
    for peer in peers:
        pl.semaphore_signal(barrier, inc=1, device_id=peer, device_id_type=MESH)

    locals_ = []

    def local(src, dst):
        copy = pltpu.make_async_copy(src, dst, lsem.at[len(locals_)])
        copy.start()
        locals_.append(copy)
        return copy

    def lanes(start, size=128):
        return pl.ds(pl.multiple_of(start, 128), size)

    mine = lanes(row * 256, 256)
    load_la_q = local(a_q, la_q)
    load_lb_o = local(b_o, lb_o)
    loads = [local(b_q, vb_q.at[0, mine, :])]
    for d in (1, 2, 3):
        to = (y + STEP[d] + 4) % 4
        loads.append(local(a_o.at[:, lanes(to * 512, 512)], sa_o.at[d - 1]))
    loads.append(local(a_o.at[:, lanes(y * 512, 512)], va_o.at[0, x]))

    def features(u):
        return pl.ds(pl.multiple_of((u + 4) % 4 * 576, 64), 576)

    load_la_q.wait()
    ta_q[...] = la_q[...].T
    at_q[:, lanes(x * 128)] = ta_q[features(z), :]
    load_lb_o.wait()
    bt_o[:, :, lanes(row * 256, 256)] = lb_o[...].T.reshape(4, 288, 256)
    for copy in loads:
        copy.wait()
    pl.semaphore_wait(barrier, len(peers))

    flows = {}

    def flow(kind, number, which, *pieces):
        flows[kind, number, which] = pieces

    ahead, behind = (x + 1) % 4, (x + 3) % 4

    def piece_q(s, c):
        return at_q.at[:, lanes(s * 512 + c * 128)]

    for d in (1, 2, 3):
        flow(EXQ, d, 0, (ta_q.at[features(z + STEP[d]), :], piece_q(d, x), on("z", STEP[d])))
        flow(EXO, d, 0, (sa_o.at[d - 1], va_o.at[d, x], on("y", STEP[d])))
    for s in range(4):
        for step in (1, -1):
            src = ta_q.at[features(z), :] if s == 0 else piece_q(s, x)
            flow(GQ, s, step, (src, piece_q(s, x), at(dx=step)))
            flow(GO, s, step, (va_o.at[s, x], va_o.at[s, x], at(dx=step)))
            came_from = behind if step == 1 else ahead
            if s < 2:
                part_q, part_o = piece_q(s, came_from), va_o.at[s, came_from]
            else:
                half = slice(0, 288) if step == 1 else slice(288, 576)
                part_q = at_q.at[half, lanes(s * 512 + came_from * 128)]
                half = slice(0, 64) if step == 1 else slice(64, 128)
                part_o = va_o.at[s, came_from, half]
            flow(HQ, s, step, (part_q, part_q, at(dx=step)))
            flow(HO, s, step, (part_o, part_o, at(dx=step)))

    order_q = [(z + 1 + s) % 4 for s in range(4)]
    halves = [lanes(row * 256 + h * 128, 128) for h in (0, 1)]

    def strip(d, rows, j):
        return vb_q.at[d, rows, lanes((j + 4) % 4 * 512, 512)]

    def same(part, device):
        return (part, part, device)

    for p in range(4):
        flow(DQ, p, 1, (strip(0, mine, z + 2 + p), strip(1, mine, z + 2 + p), at(dz=1)))
        flow(DQ, p, -1, (strip(0, mine, z + p), strip(2, mine, z + p), at(dz=-1)))
        for d in (1, 2, 3):
            flow(AQ, p, d, same(strip(d, mine, order_q[p]), sibling))
        flow(AQ, p, 0, *[same(strip(d, mine, order_q[p]), sibling) for d in (1, 2, 3)])
    flow(RQ, 0, 0, (strip(1, mine, z + 2), strip(3, mine, z + 2), at(dz=1)))
    flow(RQ, 3, 1, (strip(1, halves[0], z + 1), strip(3, halves[0], z + 1), at(dz=1)))
    flow(RQ, 3, 2, (strip(1, halves[1], z + 1), strip(3, halves[1], z + 1), at(dz=1)))
    flow(RQ, 1, 0, (strip(2, mine, z + 1), strip(3, mine, z + 1), at(dz=-1)))
    flow(RQ, 2, 0, (strip(2, mine, z + 2), strip(3, mine, z + 2), at(dz=-1)))
    flow(OWNQ, 0, 0, same(vb_q.at[0, mine, :], sibling))

    def turned(d, p, first=0, size=256):
        return bt_o.at[2 * p:2 * p + 2, :, lanes(d * 512 + row * 256 + first, size)]

    for p in (0, 1):
        for d in (1, 2):
            flow(DO, p, STEP[d], (turned(0, p), turned(d, p), at(dy=STEP[d])))
            first = (d - 1) * 128
            flow(RO, p, STEP[d], (turned(d, p, first, 128), turned(3, p, first, 128), at(dy=STEP[d])))
        flow(AO, p, 0, same(turned(1, p), sibling), same(turned(2, p), sibling))
        flow(AO, p + 2, 0, same(turned(3, p), sibling))
    own = bt_o.at[:, :, lanes(row * 256, 256)]
    flow(OWNO, 0, 0, same(own, sibling))

    order_o = [(y + 1 + s) % 4 for s in range(4)]

    def part_q(s, w, h):
        return c_q.at[order_q[s], (w + 4) % 4, h]

    def part_o(s, w, h):
        return c_o.at[(w + 4) % 4, order_o[s], h]

    for s in range(4):
        for axis, w, part, r1, r2, (far, near, late) in (
            ("y", y, part_q, r1_q, r2_q, (PQ, IQ, LQ)),
            ("z", z, part_o, r1_o, r2_o, (PO, IO, LO)),
        ):
            up, down = on(axis, 1), on(axis, -1)
            flow(far, s, 1, (part(s, w + 2, 0), r1.at[s, 0], up))
            flow(far, s, -1, (part(s, w + 2, 1), r1.at[s, 1], down))
            flow(near, s, 1, (part(s, w + 1, 1), r2.at[s, 0, 1], up))
            flow(near, s, -1, (part(s, w - 1, 0), r2.at[s, 1, 0], down))
            flow(late, s, 1, (part(s, w + 1, 0), r2.at[s, 0, 0], up))
            flow(late, s, -1, (part(s, w - 1, 1), r2.at[s, 1, 1], down))
    home_q = out_q.at[features(z), :]
    home_o = out_o.at[:, lanes(y * 512, 512)]
    for s in range(3):
        flow(FQ, s, 0, (f_q.at[s], home_q, (row, x, order_q[s] * 4 + y)))
        flow(FO, s, 0, (f_o.at[s], home_o, (row, x, z * 4 + order_o[s])))

    def multiply_q(s):
        j = order_q[s]

        @pl.loop(0, 2)
        def _(n):
            right = vb_q[:, :, lanes(j * 512 + n * 256, 256)].reshape(2048, 256)
            total = jnp.dot(at_q[...], right, preferred_element_type=F32)
            for c in (0, 1):
                for h in (0, 1):
                    c_q[j, 2 * n + c, h] = total[h * 288:(h + 1) * 288, c * 128:(c + 1) * 128]

    def multiply_o(first):
        slots, k = (slice(0, 2), slice(0, 1024)) if first else (slice(2, 4), slice(1024, 2048))

        @pl.loop(0, 4)
        def _(w):
            for h in (0, 1):
                right = va_o[slots, :, :, h * 256:(h + 1) * 256].reshape(1024, 256)
                total = jnp.dot(bt_o[w, :, k], right, preferred_element_type=F32)
                for j in range(4):
                    part = total[j * 72:(j + 1) * 72]
                    c_o[w, j, h] = part if first else c_o[w, j, h] + part

    def join(s, w, part, r1):
        for ref, k in ((part(s, w + 1, 0), 0), (part(s, w - 1, 1), 1)):
            ref[...] = ref[...] + r1[s, k]

    def join_q(s):
        join(s, y, part_q, r1_q)

    def join_o(s):
        join(s, z, part_o, r1_o)

    def finish_q(s):
        for h in (0, 1):
            rows = slice(h * 288, (h + 1) * 288)
            total = part_q(s, y, h)[...] + r2_q[s, 0, h] + r2_q[s, 1, h]
            if s < 3:
                f_q[s, rows] = total
            else:
                out_q[pl.ds(pl.multiple_of(z * 576 + h * 288, 32), 288)] = total

    def finish_o(s):
        for h in (0, 1):
            total = part_o(s, z, h)[...] + r2_o[s, 0, h] + r2_o[s, 1, h]
            if s < 3:
                f_o[s, :, h * 256:(h + 1) * 256] = total
            else:
                out_o[:, lanes(y * 512 + h * 256, 256)] = total

    copies, n_sent = {}, [0]
    open_left, open_came = {}, {}

    def send(*names):
        for name in names:
            copies[name] = []
            for src, dst, device in flows[name]:
                k = n_sent[0]
                n_sent[0] += 1
                copy = pltpu.make_async_remote_copy(
                    src, dst, ssem.at[k], rsem.at[k], device_id=device, device_id_type=MESH
                )
                copy.start()
                copies[name].append(copy)
            open_left[name] = open_came[name] = True

    def left(*names):
        for name in names:
            del open_left[name]
            for copy in copies[name]:
                copy.wait_send()

    def came(*names):
        for name in names:
            del open_came[name]
            for copy in copies[name]:
                copy.wait_recv()

    send((EXO, 1, 0), (EXO, 2, 0))
    send((EXQ, 1, 0), (EXQ, 2, 0))
    send((GQ, 0, 1), (GQ, 0, -1))
    left((EXO, 1, 0), (EXO, 2, 0))
    send((EXO, 3, 0))
    send((EXQ, 3, 0))
    came((EXQ, 2, 0))
    send((GQ, 2, 1), (GQ, 2, -1))
    send((OWNQ, 0, 0), (OWNO, 0, 0))
    left((EXQ, 1, 0), (EXQ, 2, 0))
    send((DQ, 0, 1), (DQ, 0, -1))
    left((EXO, 3, 0))
    send((DO, 0, 1), (DO, 0, -1))
    left((GQ, 0, 1))
    came((EXQ, 1, 0))
    send((GQ, 1, 1), (GQ, 1, -1))
    came((EXQ, 3, 0))
    send((GQ, 3, 1), (GQ, 3, -1))
    left((DQ, 0, 1))
    send((DQ, 1, 1))
    left((GQ, 1, 1))
    came((GQ, 0, 1))
    send((HQ, 0, 1))
    left((DO, 0, 1), (DO, 0, -1))
    send((DO, 1, 1), (DO, 1, -1))
    left((GQ, 1, -1))
    came((GQ, 1, -1))
    send((HQ, 1, -1))
    left((DQ, 0, -1))
    send((DQ, 1, -1))
    left((HQ, 0, 1))
    came((GQ, 2, 1), (GQ, 2, -1))
    send((HQ, 2, 1), (HQ, 2, -1))
    came((DQ, 0, -1), (DQ, 0, 1))
    send((AQ, 0, 1), (AQ, 0, 2))
    send((RQ, 1, 0))
    came((EXO, 3, 0))
    send((GO, 3, 1), (GO, 3, -1))
    came((DQ, 1, 1))
    send((RQ, 0, 0), (AQ, 1, 1))
    came((EXO, 1, 0))
    send((GO, 1, 1), (GO, 1, -1))
    came((GQ, 3, 1), (GQ, 3, -1))
    send((HQ, 3, 1), (HQ, 3, -1))
    came((DO, 0, 1), (DO, 0, -1))
    send((RO, 0, 1), (RO, 0, -1), (AO, 0, 0))
    came((DO, 1, 1), (DO, 1, -1))
    send((RO, 1, 1), (RO, 1, -1), (AO, 1, 0))
    left((RQ, 0, 0))
    send((DQ, 2, 1))
    send((GO, 0, 1), (GO, 0, -1))
    left((DQ, 1, -1), (RQ, 1, 0))
    send((DQ, 2, -1))
    came((RQ, 0, 0))
    send((AQ, 0, 3))
    came((RO, 1, 1), (RO, 1, -1))
    send((AO, 3, 0))
    send((RQ, 3, 2))
    came((DQ, 1, -1))
    send((AQ, 1, 2))
    send((RQ, 2, 0))
    came((RQ, 1, 0))
    send((AQ, 1, 3))
    came((EXO, 2, 0))
    send((GO, 2, 1), (GO, 2, -1))
    came((GO, 3, 1), (GO, 3, -1))
    send((HO, 3, 1), (HO, 3, -1))
    came((GQ, 0, -1), (HQ, 0, 1), (GQ, 1, 1), (HQ, 1, -1), (HQ, 2, 1), (HQ, 2, -1), (HQ, 3, 1), (HQ, 3, -1))
    came((AQ, 0, 1), (AQ, 0, 2), (AQ, 0, 3), (OWNQ, 0, 0))
    multiply_q(0)
    send((PQ, 0, 1), (PQ, 0, -1))
    came((GO, 1, -1))
    send((HO, 1, -1))
    left((DQ, 1, 1))
    send((RQ, 3, 1))
    came((RO, 0, 1), (RO, 0, -1))
    send((AO, 2, 0))
    came((AQ, 1, 1), (AQ, 1, 2), (AQ, 1, 3))
    multiply_q(1)
    send((PQ, 1, 1), (PQ, 1, -1))
    left((GO, 1, 1))
    came((GO, 0, 1))
    send((HO, 0, 1))
    left((DQ, 2, -1))
    send((DQ, 3, -1))
    send((IQ, 0, 1), (IQ, 0, -1))
    left((DQ, 2, 1), (RQ, 3, 2))
    send((DQ, 3, 1))
    send((IQ, 1, 1), (IQ, 1, -1))
    came((GO, 2, 1), (GO, 2, -1))
    send((HO, 2, 1), (HO, 2, -1))
    came((OWNO, 0, 0), (AO, 0, 0), (AO, 1, 0), (AO, 2, 0), (AO, 3, 0), (GO, 0, -1), (HO, 0, 1), (GO, 1, 1))
    came((HO, 1, -1))
    multiply_o(True)
    came((PQ, 0, 1), (PQ, 0, -1))
    join_q(0)
    send((LQ, 0, 1), (LQ, 0, -1))
    came((HO, 2, 1), (HO, 2, -1), (HO, 3, 1), (HO, 3, -1))
    multiply_o(False)
    send((PO, 3, 1), (PO, 3, -1), (IO, 3, 1), (IO, 3, -1))
    came((DQ, 2, 1), (DQ, 2, -1), (RQ, 2, 0))
    send((AQ, 2, 0))
    came((DQ, 3, 1), (DQ, 3, -1), (RQ, 3, 1), (RQ, 3, 2))
    send((AQ, 3, 0))
    send((PO, 2, 1), (PO, 2, -1), (IO, 2, 1), (IO, 2, -1))
    send((PO, 0, 1), (PO, 0, -1), (IO, 0, 1), (IO, 0, -1))
    came((PQ, 1, 1), (PQ, 1, -1))
    join_q(1)
    send((LQ, 1, 1), (LQ, 1, -1))
    came((AQ, 2, 0))
    multiply_q(2)
    send((PQ, 2, 1), (PQ, 2, -1))
    came((PO, 3, 1), (PO, 3, -1))
    join_o(3)
    send((LO, 3, 1), (LO, 3, -1))
    send((IQ, 2, 1), (IQ, 2, -1))
    came((IQ, 1, 1), (IQ, 1, -1), (LQ, 1, 1), (LQ, 1, -1))
    finish_q(1)
    send((FQ, 1, 0))
    came((AQ, 3, 0))
    multiply_q(3)
    send((PQ, 3, 1), (PQ, 3, -1))
    left((PO, 0, 1))
    send((PO, 1, 1), (PO, 1, -1), (IO, 1, 1), (IO, 1, -1))
    came((IO, 3, 1), (IO, 3, -1), (LO, 3, 1), (LO, 3, -1))
    finish_o(3)
    came((PQ, 2, 1), (PQ, 2, -1))
    join_q(2)
    send((LQ, 2, 1), (LQ, 2, -1))
    came((PO, 0, 1), (PO, 0, -1))
    join_o(0)
    send((LO, 0, 1), (LO, 0, -1))
    left((PQ, 3, 1))
    send((IQ, 3, 1), (IQ, 3, -1))
    came((PO, 2, 1), (PO, 2, -1))
    join_o(2)
    send((LO, 2, 1), (LO, 2, -1))
    came((PO, 1, 1), (PO, 1, -1))
    join_o(1)
    send((LO, 1, 1), (LO, 1, -1))
    came((PQ, 3, 1), (PQ, 3, -1))
    join_q(3)
    send((LQ, 3, 1), (LQ, 3, -1))
    came((IQ, 2, 1), (IQ, 2, -1), (LQ, 2, 1), (LQ, 2, -1))
    finish_q(2)
    send((FQ, 2, 0))
    came((IQ, 0, 1), (IQ, 0, -1), (LQ, 0, 1), (LQ, 0, -1))
    finish_q(0)
    send((FQ, 0, 0))
    came((IO, 2, 1), (IO, 2, -1), (LO, 2, 1), (LO, 2, -1))
    finish_o(2)
    send((FO, 2, 0))
    came((IO, 0, 1), (IO, 0, -1), (LO, 0, 1), (LO, 0, -1))
    finish_o(0)
    send((FO, 0, 0))
    came((IQ, 3, 1), (IQ, 3, -1), (LQ, 3, 1), (LQ, 3, -1))
    finish_q(3)
    came((IO, 1, 1), (IO, 1, -1), (LO, 1, 1), (LO, 1, -1))
    finish_o(1)
    send((FO, 1, 0))

    came(*list(open_came))
    left(*list(open_left))
    assert n_sent[0] <= N_SEM and len(locals_) == 7, (n_sent, len(locals_))


def per_device(normed, qkv_grad, attn_out, out_grad):
    flat = [v.reshape(v.shape[0] * v.shape[1], v.shape[2]) for v in (normed, qkv_grad, attn_out, out_grad)]
    hbm = pl.BlockSpec(memory_space=pltpu.HBM)
    vmem = pl.BlockSpec(memory_space=pltpu.VMEM)
    out_q, out_o = pl.pallas_call(
        kernel,
        out_shape=(
            jax.ShapeDtypeStruct((2304, 128), F32),
            jax.ShapeDtypeStruct((72, 2048), F32),
        ),
        in_specs=[hbm] * 4,
        out_specs=[vmem] * 2,
        scratch_shapes=[
            pltpu.VMEM((128, 2304), BF16),
            pltpu.VMEM((2304, 128), BF16),
            pltpu.VMEM((576, 2048), BF16),
            pltpu.VMEM((4, 512, 2048), BF16),
            pltpu.VMEM((4, 4, 2, 288, 128), F32),
            pltpu.VMEM((4, 2, 288, 128), F32),
            pltpu.VMEM((4, 2, 2, 288, 128), F32),
            pltpu.VMEM((3, 576, 128), F32),
            pltpu.VMEM((3, 128, 512), BF16),
            pltpu.VMEM((4, 4, 128, 512), BF16),
            pltpu.VMEM((256, 1152), BF16),
            pltpu.VMEM((4, 288, 2048), BF16),
            pltpu.VMEM((4, 4, 2, 72, 256), F32),
            pltpu.VMEM((4, 2, 72, 256), F32),
            pltpu.VMEM((4, 2, 2, 72, 256), F32),
            pltpu.VMEM((3, 72, 512), F32),
            pltpu.SemaphoreType.DMA((N_SEM,)),
            pltpu.SemaphoreType.DMA((N_SEM,)),
            pltpu.SemaphoreType.DMA((7,)),
        ],
        compiler_params=pltpu.CompilerParams(
            collective_id=0, has_side_effects=True, vmem_limit_bytes=40 * 1024 * 1024
        ),
        name="weight_grads",
    )(*[pltpu.with_memory_space_constraint(v, pltpu.HBM) for v in flat])
    return out_q, out_o.T


def solution(mesh):
    in_specs = (
        P("col", "depth", "row"),
        P("row", "depth", "col"),
        P("col", "depth", "row"),
        P("row", "depth", "col"),
    )
    out_specs = (P("row", ("col", "depth")), P("row", ("col", "depth")))
    return jax.shard_map(
        per_device, mesh=mesh, in_specs=in_specs, out_specs=out_specs, check_vma=False
    )
```

time: 270 us -> 90.6 us (0.34)
  waiting for transfers between devices: 165 us -> 0 us
  Pallas kernels: 0 us -> 87.9 us
  blocking collectives: 73.3 us -> 0 us
  matrix products: 14.4 us -> 0 us
  between operations: 14.1 us -> 0.64 us
    reduce_scatter x1 -> x0, waiting for transfers between devices: 125 us -> none  [qkv_total(): lax.psum_scatter(partial_qkv, 'depth', scatter_dimension=1, tiled=True)]
    pallas_call x0 -> x1, Pallas kernels: none -> 87.9 us  [per_device(): pl.pallas_call(kernel, out_shape=(jax.ShapeDtypeStruct((2304, 128), F32),...]
    all_to_all x4 -> x0, blocking collectives: 73.3 us -> none  [sent_to_all(): lax.all_to_all(jnp.broadcast_to(x[None], (peers, *x.shape)), axis, 0, 0,...]
    unnamed x3 -> x0, waiting for transfers between devices: 40.2 us -> none
    dot_general x2 -> x0, matrix products: 14.4 us -> none  [outer_sum(): lax.dot_general(left, right, (((0,), (0,)), ((), ())), preferred_element_...]
  transfers between devices with their start and end apart: 2 -> 0, of which waited for: 2 -> 0; matrix products, arithmetic and copies ran while one was open for 4% -> 0% of each run, Pallas kernels for 0% -> 0%
where the time goes in v2:
time: 90.6 us; the launch traced here: 90.4 us
  Pallas kernels  87.9 us (97%)
  local copies, waits for them, and re-layouts  1.83 us (2%)
    pallas_call x1, Pallas kernels, per_device(): pl.pallas_call(kernel, out_shape=(jax.ShapeDtypeStruct((2304, 128), F32),...  87.9 us
    unnamed x2, local copies, waits for them, and re-layouts  1.83 us

profile of v2, /device:TPU:0, one launch (start us, length us, event | category | flops | bytes accessed | tf_op | source)
XLA Modules:
  0.0 90.4 jit_solution(15069259334794255807)
XLA Ops:
  0.6 87.9 %weight_grads.1 = (f32[2304,128]{1,0:T(8,128)S(1)}, f32[72,2048]{1,0:T(8,128)S(1)}) custom-call(bf16[128,2304]{1,0:T(8,128)(2,1)} %bitcast.7, bf16[256,2048]{1,0:T(8,128)(2,1)} %bitcast.6, bf16[128,2048]{1,0:T(8,128)(2,1)} %bitcast.9, bf16[256,1152]{1,0:T(8,128)(2,1)} %bitcast.8), custom_call_target="tpu_custom_call" | custom-call | tf_op jit(solution)/shard_map/weight_grads/pallas_call | solution.py:411
  88.6 1.0 %copy.8 = f32[2304,128]{1,0:T(8,128)} copy(f32[2304,128]{1,0:T(8,128)S(1)} %get-tuple-element.8) | data formatting | bytes 2359296
  89.6 0.8 copy.9

commit v3 on v2

--- a/solution.py
+++ b/solution.py
@@ -11,7 +11,7 @@
 
 (EXQ, EXO, GQ, GO, HQ, HO, OWNQ, OWNO, DQ, DO, RQ, RO, AQ, AO, PQ, PO, IQ, IO, LQ, LO, FQ, FO) = range(22)
 STEP = {1: 1, 2: -1, 3: 2}
-N_SEM = 180
+N_SEND, N_COME = 27, 96
 
 
 def kernel(
@@ -114,7 +114,10 @@
         for d in (1, 2, 3):
             flow(AQ, p, d, same(strip(d, mine, order_q[p]), sibling))
         flow(AQ, p, 0, *[same(strip(d, mine, order_q[p]), sibling) for d in (1, 2, 3)])
-    flow(RQ, 0, 0, (strip(1, mine, z + 2), strip(3, mine, z + 2), at(dz=1)))
+    for h in (0, 1):
+        flow(DQ, 1, h + 2, (strip(0, halves[h], z + 3), strip(1, halves[h], z + 3), at(dz=1)))
+        flow(RQ, 0, h, (strip(1, halves[h], z + 2), strip(3, halves[h], z + 2), at(dz=1)))
+        flow(AQ, 0, h + 4, same(strip(3, halves[h], order_q[0]), sibling))
     flow(RQ, 3, 1, (strip(1, halves[0], z + 1), strip(3, halves[0], z + 1), at(dz=1)))
     flow(RQ, 3, 2, (strip(1, halves[1], z + 1), strip(3, halves[1], z + 1), at(dz=1)))
     flow(RQ, 1, 0, (strip(2, mine, z + 1), strip(3, mine, z + 1), at(dz=-1)))
@@ -210,198 +213,254 @@
             else:
                 out_o[:, lanes(y * 512 + h * 256, 256)] = total
 
-    copies, n_sent = {}, [0]
+    whole = {}
+    for s in range(4):
+        for p, i, l, r1, r2 in ((PQ, IQ, LQ, r1_q, r2_q), (PO, IO, LO, r1_o, r2_o)):
+            far, rest = r1.at[s], r2.at[s]
+            for step in (1, -1):
+                whole[p, s, step] = far
+                whole[i, s, step] = whole[l, s, step] = rest
+    for p in (2, 3):
+        whole[AQ, p, 0] = vb_q.at[1:4, mine, lanes(order_q[p] * 512, 512)]
+    copies, arrivals, free = {}, {}, list(range(N_SEND))
     open_left, open_came = {}, {}
 
     def send(*names):
         for name in names:
             copies[name] = []
             for src, dst, device in flows[name]:
-                k = n_sent[0]
-                n_sent[0] += 1
+                group = id(whole[name]) if name in whole else (name, len(copies[name]))
+                arrival = arrivals.setdefault(group, len(arrivals))
+                k = free.pop(0)
                 copy = pltpu.make_async_remote_copy(
-                    src, dst, ssem.at[k], rsem.at[k], device_id=device, device_id_type=MESH
+                    src, dst, ssem.at[k], rsem.at[arrival], device_id=device, device_id_type=MESH
                 )
                 copy.start()
-                copies[name].append(copy)
+                copies[name].append((copy, k))
             open_left[name] = open_came[name] = True
 
     def left(*names):
         for name in names:
             del open_left[name]
-            for copy in copies[name]:
+            for copy, k in copies[name]:
                 copy.wait_send()
+                free.append(k)
 
     def came(*names):
         for name in names:
-            del open_came[name]
-            for copy in copies[name]:
-                copy.wait_recv()
-
-    send((EXO, 1, 0), (EXO, 2, 0))
+            if name not in open_came:
+                continue
+            if name in whole:
+                both = whole[name]
+                arrival = arrivals[id(both)]
+                pltpu.make_async_remote_copy(
+                    both, both, ssem.at[0], rsem.at[arrival], device_id=sibling, device_id_type=MESH
+                ).wait_recv()
+                for other in whole:
+                    if whole[other] is both:
+                        del open_came[other]
+            else:
+                del open_came[name]
+                for copy, _ in copies[name]:
+                    copy.wait_recv()
+
     send((EXQ, 1, 0), (EXQ, 2, 0))
     send((GQ, 0, 1), (GQ, 0, -1))
-    left((EXO, 1, 0), (EXO, 2, 0))
     send((EXO, 3, 0))
+    left((EXQ, 1, 0), (EXQ, 2, 0))
     send((EXQ, 3, 0))
     came((EXQ, 2, 0))
     send((GQ, 2, 1), (GQ, 2, -1))
-    send((OWNQ, 0, 0), (OWNO, 0, 0))
-    left((EXQ, 1, 0), (EXQ, 2, 0))
-    send((DQ, 0, 1), (DQ, 0, -1))
     left((EXO, 3, 0))
     send((DO, 0, 1), (DO, 0, -1))
-    left((GQ, 0, 1))
+    left((GQ, 0, 1), (GQ, 0, -1))
+    left((EXQ, 3, 0))
+    send((DQ, 0, 1), (DQ, 0, -1))
+    send((EXO, 1, 0), (EXO, 2, 0))
     came((EXQ, 1, 0))
     send((GQ, 1, 1), (GQ, 1, -1))
+    left((GQ, 2, 1))
     came((EXQ, 3, 0))
     send((GQ, 3, 1), (GQ, 3, -1))
-    left((DQ, 0, 1))
-    send((DQ, 1, 1))
-    left((GQ, 1, 1))
+    send((OWNQ, 0, 0), (OWNO, 0, 0))
+    send((DQ, 1, 2))
+    left((DQ, 0, -1))
+    send((DQ, 1, -1))
+    left((GQ, 2, -1))
+    came((DQ, 0, -1))
+    send((RQ, 1, 0))
+    send((DQ, 1, 3))
+    came((GQ, 2, 1), (GQ, 2, -1))
+    send((HQ, 2, 1), (HQ, 2, -1))
+    left((EXO, 1, 0), (EXO, 2, 0), (GQ, 1, 1), (GQ, 1, -1))
+    came((GQ, 1, -1))
+    send((HQ, 1, -1))
+    came((EXO, 1, 0))
+    send((GO, 1, 1), (GO, 1, -1))
     came((GQ, 0, 1))
     send((HQ, 0, 1))
+    left((OWNO, 0, 0))
     left((DO, 0, 1), (DO, 0, -1))
     send((DO, 1, 1), (DO, 1, -1))
-    left((GQ, 1, -1))
-    came((GQ, 1, -1))
-    send((HQ, 1, -1))
-    left((DQ, 0, -1))
-    send((DQ, 1, -1))
-    left((HQ, 0, 1))
-    came((GQ, 2, 1), (GQ, 2, -1))
-    send((HQ, 2, 1), (HQ, 2, -1))
-    came((DQ, 0, -1), (DQ, 0, 1))
+    came((DQ, 1, 2))
+    send((RQ, 0, 0))
+    came((DO, 0, 1), (DO, 0, -1))
+    send((RO, 0, 1), (RO, 0, -1), (AO, 0, 0))
+    left((DQ, 0, 1), (GQ, 3, -1), (OWNQ, 0, 0), (DQ, 1, 2))
+    came((DQ, 1, 3))
+    send((RQ, 0, 1), (AQ, 1, 1))
+    send((GO, 0, 1), (GO, 0, -1))
+    came((DQ, 0, 1))
     send((AQ, 0, 1), (AQ, 0, 2))
-    send((RQ, 1, 0))
+    came((GQ, 3, 1), (GQ, 3, -1))
+    send((HQ, 3, 1), (HQ, 3, -1))
+    left((DQ, 1, 3), (HQ, 2, 1), (HQ, 2, -1))
+    came((DQ, 1, -1))
+    send((AQ, 1, 2))
+    came((RQ, 0, 0))
+    send((AQ, 0, 4))
+    left((RQ, 0, 1))
+    send((RQ, 3, 1))
+    left((RQ, 1, 0))
+    send((RQ, 2, 0))
+    left((GO, 1, -1), (AO, 0, 0), (AQ, 1, 1), (AQ, 0, 1), (AQ, 0, 2))
+    came((RQ, 0, 1))
+    send((AQ, 0, 5))
+    left((RQ, 0, 0))
+    send((DQ, 2, 1))
+    left((GQ, 3, 1))
+    came((EXO, 2, 0))
+    send((GO, 2, 1), (GO, 2, -1))
+    send((RQ, 3, 2))
     came((EXO, 3, 0))
     send((GO, 3, 1), (GO, 3, -1))
-    came((DQ, 1, 1))
-    send((RQ, 0, 0), (AQ, 1, 1))
-    came((EXO, 1, 0))
-    send((GO, 1, 1), (GO, 1, -1))
-    came((GQ, 3, 1), (GQ, 3, -1))
-    send((HQ, 3, 1), (HQ, 3, -1))
-    came((DO, 0, 1), (DO, 0, -1))
-    send((RO, 0, 1), (RO, 0, -1), (AO, 0, 0))
+    left((DQ, 1, -1))
+    send((DQ, 2, -1))
+    left((HQ, 1, -1), (HQ, 0, 1), (DO, 1, 1), (DO, 1, -1), (RO, 0, 1), (RO, 0, -1))
+    came((RQ, 1, 0))
+    send((AQ, 1, 3))
     came((DO, 1, 1), (DO, 1, -1))
     send((RO, 1, 1), (RO, 1, -1), (AO, 1, 0))
-    left((RQ, 0, 0))
-    send((DQ, 2, 1))
-    send((GO, 0, 1), (GO, 0, -1))
-    left((DQ, 1, -1), (RQ, 1, 0))
-    send((DQ, 2, -1))
-    came((RQ, 0, 0))
-    send((AQ, 0, 3))
-    came((RO, 1, 1), (RO, 1, -1))
-    send((AO, 3, 0))
-    send((RQ, 3, 2))
-    came((DQ, 1, -1))
-    send((AQ, 1, 2))
-    send((RQ, 2, 0))
-    came((RQ, 1, 0))
-    send((AQ, 1, 3))
-    came((EXO, 2, 0))
-    send((GO, 2, 1), (GO, 2, -1))
-    came((GO, 3, 1), (GO, 3, -1))
-    send((HO, 3, 1), (HO, 3, -1))
     came((GQ, 0, -1), (HQ, 0, 1), (GQ, 1, 1), (HQ, 1, -1), (HQ, 2, 1), (HQ, 2, -1), (HQ, 3, 1), (HQ, 3, -1))
-    came((AQ, 0, 1), (AQ, 0, 2), (AQ, 0, 3), (OWNQ, 0, 0))
+    came((AQ, 0, 1), (AQ, 0, 2), (AQ, 0, 4), (AQ, 0, 5), (OWNQ, 0, 0))
     multiply_q(0)
     send((PQ, 0, 1), (PQ, 0, -1))
-    came((GO, 1, -1))
-    send((HO, 1, -1))
-    left((DQ, 1, 1))
-    send((RQ, 3, 1))
-    came((RO, 0, 1), (RO, 0, -1))
-    send((AO, 2, 0))
     came((AQ, 1, 1), (AQ, 1, 2), (AQ, 1, 3))
     multiply_q(1)
     send((PQ, 1, 1), (PQ, 1, -1))
+    came((GO, 1, -1))
+    send((HO, 1, -1))
+    left((GO, 0, 1), (GO, 0, -1), (HQ, 3, 1), (HQ, 3, -1), (AQ, 1, 2), (AQ, 0, 4))
+    came((RO, 1, 1), (RO, 1, -1))
+    send((AO, 3, 0))
     left((GO, 1, 1))
     came((GO, 0, 1))
     send((HO, 0, 1))
+    left((AQ, 0, 5), (AQ, 1, 3), (RO, 1, 1), (RO, 1, -1), (AO, 1, 0))
+    came((GO, 3, 1), (GO, 3, -1))
+    send((HO, 3, 1), (HO, 3, -1))
+    left((PQ, 0, 1))
+    send((IQ, 0, 1), (IQ, 0, -1))
+    came((RO, 0, 1), (RO, 0, -1))
+    send((AO, 2, 0))
+    left((RQ, 3, 1), (GO, 2, 1), (GO, 2, -1), (RQ, 3, 2), (GO, 3, 1), (GO, 3, -1), (AO, 3, 0))
     left((DQ, 2, -1))
     send((DQ, 3, -1))
-    send((IQ, 0, 1), (IQ, 0, -1))
-    left((DQ, 2, 1), (RQ, 3, 2))
+    send((IQ, 1, 1), (IQ, 1, -1))
+    left((DQ, 2, 1))
     send((DQ, 3, 1))
-    send((IQ, 1, 1), (IQ, 1, -1))
     came((GO, 2, 1), (GO, 2, -1))
     send((HO, 2, 1), (HO, 2, -1))
+    left((RQ, 2, 0), (PQ, 0, -1))
     came((OWNO, 0, 0), (AO, 0, 0), (AO, 1, 0), (AO, 2, 0), (AO, 3, 0), (GO, 0, -1), (HO, 0, 1), (GO, 1, 1))
     came((HO, 1, -1))
     multiply_o(True)
+    came((DQ, 2, 1), (DQ, 2, -1), (RQ, 2, 0))
+    send((AQ, 2, 0))
     came((PQ, 0, 1), (PQ, 0, -1))
     join_q(0)
     send((LQ, 0, 1), (LQ, 0, -1))
+    left((PQ, 1, 1), (PQ, 1, -1), (HO, 1, -1), (HO, 0, 1), (HO, 3, 1), (HO, 3, -1), (AO, 2, 0), (HO, 2, 1))
+    left((HO, 2, -1))
     came((HO, 2, 1), (HO, 2, -1), (HO, 3, 1), (HO, 3, -1))
     multiply_o(False)
-    send((PO, 3, 1), (PO, 3, -1), (IO, 3, 1), (IO, 3, -1))
-    came((DQ, 2, 1), (DQ, 2, -1), (RQ, 2, 0))
-    send((AQ, 2, 0))
-    came((DQ, 3, 1), (DQ, 3, -1), (RQ, 3, 1), (RQ, 3, 2))
-    send((AQ, 3, 0))
-    send((PO, 2, 1), (PO, 2, -1), (IO, 2, 1), (IO, 2, -1))
-    send((PO, 0, 1), (PO, 0, -1), (IO, 0, 1), (IO, 0, -1))
+    send((PO, 2, 1), (PO, 2, -1))
+    send((PO, 3, 1), (PO, 3, -1))
+    send((IO, 3, 1), (IO, 3, -1))
     came((PQ, 1, 1), (PQ, 1, -1))
     join_q(1)
     send((LQ, 1, 1), (LQ, 1, -1))
+    came((DQ, 3, 1), (DQ, 3, -1), (RQ, 3, 1), (RQ, 3, 2))
+    send((AQ, 3, 0))
     came((AQ, 2, 0))
     multiply_q(2)
     send((PQ, 2, 1), (PQ, 2, -1))
+    send((PO, 0, 1), (PO, 0, -1))
+    left((IQ, 0, 1), (IQ, 0, -1), (DQ, 3, -1), (IQ, 1, 1), (IQ, 1, -1), (DQ, 3, 1), (AQ, 2, 0))
+    left((PO, 2, 1))
+    send((IO, 2, 1), (IO, 2, -1))
     came((PO, 3, 1), (PO, 3, -1))
     join_o(3)
     send((LO, 3, 1), (LO, 3, -1))
+    came((AQ, 3, 0))
+    multiply_q(3)
+    send((PQ, 3, 1), (PQ, 3, -1))
     send((IQ, 2, 1), (IQ, 2, -1))
+    left((PO, 0, 1))
+    send((PO, 1, 1), (PO, 1, -1))
+    left((LQ, 0, 1), (LQ, 0, -1), (PO, 2, -1), (PO, 3, 1), (PO, 3, -1), (IO, 3, 1), (IO, 3, -1), (AQ, 3, 0))
+    left((PO, 0, -1))
     came((IQ, 1, 1), (IQ, 1, -1), (LQ, 1, 1), (LQ, 1, -1))
     finish_q(1)
     send((FQ, 1, 0))
-    came((AQ, 3, 0))
-    multiply_q(3)
-    send((PQ, 3, 1), (PQ, 3, -1))
-    left((PO, 0, 1))
-    send((PO, 1, 1), (PO, 1, -1), (IO, 1, 1), (IO, 1, -1))
+    came((PO, 0, 1), (PO, 0, -1))
+    join_o(0)
+    send((LO, 0, 1), (LO, 0, -1))
+    came((PO, 2, 1), (PO, 2, -1))
+    join_o(2)
+    send((LO, 2, 1), (LO, 2, -1))
+    left((LQ, 1, 1), (LQ, 1, -1), (IO, 2, 1), (IO, 2, -1))
     came((IO, 3, 1), (IO, 3, -1), (LO, 3, 1), (LO, 3, -1))
     finish_o(3)
+    left((PQ, 2, 1), (PQ, 2, -1), (LO, 3, 1), (LO, 3, -1))
     came((PQ, 2, 1), (PQ, 2, -1))
     join_q(2)
     send((LQ, 2, 1), (LQ, 2, -1))
-    came((PO, 0, 1), (PO, 0, -1))
-    join_o(0)
-    send((LO, 0, 1), (LO, 0, -1))
-    left((PQ, 3, 1))
-    send((IQ, 3, 1), (IQ, 3, -1))
-    came((PO, 2, 1), (PO, 2, -1))
-    join_o(2)
-    send((LO, 2, 1), (LO, 2, -1))
+    send((IO, 0, 1), (IO, 0, -1))
+    send((IO, 1, 1), (IO, 1, -1))
     came((PO, 1, 1), (PO, 1, -1))
     join_o(1)
     send((LO, 1, 1), (LO, 1, -1))
+    left((PO, 1, 1), (PO, 1, -1))
+    left((PQ, 3, 1))
+    send((IQ, 3, 1), (IQ, 3, -1))
+    came((IQ, 0, 1), (IQ, 0, -1), (LQ, 0, 1), (LQ, 0, -1))
+    finish_q(0)
+    send((FQ, 0, 0))
     came((PQ, 3, 1), (PQ, 3, -1))
     join_q(3)
     send((LQ, 3, 1), (LQ, 3, -1))
+    left((PQ, 3, -1), (IQ, 2, 1), (IQ, 2, -1), (LO, 0, 1), (LO, 0, -1), (LO, 2, 1), (LO, 2, -1))
     came((IQ, 2, 1), (IQ, 2, -1), (LQ, 2, 1), (LQ, 2, -1))
     finish_q(2)
     send((FQ, 2, 0))
-    came((IQ, 0, 1), (IQ, 0, -1), (LQ, 0, 1), (LQ, 0, -1))
-    finish_q(0)
-    send((FQ, 0, 0))
+    left((LQ, 2, 1), (LQ, 2, -1), (IO, 0, 1), (IO, 0, -1), (IO, 1, 1), (IO, 1, -1))
+    came((IO, 1, 1), (IO, 1, -1), (LO, 1, 1), (LO, 1, -1))
+    finish_o(1)
+    send((FO, 1, 0))
+    came((IO, 0, 1), (IO, 0, -1), (LO, 0, 1), (LO, 0, -1))
+    finish_o(0)
+    send((FO, 0, 0))
     came((IO, 2, 1), (IO, 2, -1), (LO, 2, 1), (LO, 2, -1))
     finish_o(2)
     send((FO, 2, 0))
-    came((IO, 0, 1), (IO, 0, -1), (LO, 0, 1), (LO, 0, -1))
-    finish_o(0)
-    send((FO, 0, 0))
+    left((LO, 1, 1), (LO, 1, -1))
     came((IQ, 3, 1), (IQ, 3, -1), (LQ, 3, 1), (LQ, 3, -1))
     finish_q(3)
-    came((IO, 1, 1), (IO, 1, -1), (LO, 1, 1), (LO, 1, -1))
-    finish_o(1)
-    send((FO, 1, 0))
 
     came(*list(open_came))
     left(*list(open_left))
-    assert n_sent[0] <= N_SEM and len(locals_) == 7, (n_sent, len(locals_))
+    assert len(arrivals) == N_COME and len(locals_) == 7, len(arrivals)
 
 
 def per_device(normed, qkv_grad, attn_out, out_grad):
@@ -433,8 +492,8 @@
             pltpu.VMEM((4, 2, 72, 256), F32),
             pltpu.VMEM((4, 2, 2, 72, 256), F32),
             pltpu.VMEM((3, 72, 512), F32),
-            pltpu.SemaphoreType.DMA((N_SEM,)),
-            pltpu.SemaphoreType.DMA((N_SEM,)),
+            pltpu.SemaphoreType.DMA((N_SEND,)),
+            pltpu.SemaphoreType.DMA((N_COME,)),
             pltpu.SemaphoreType.DMA((7,)),
         ],
         compiler_params=pltpu.CompilerParams(

time: 90.6 us -> 88.3 us (0.975)
  Pallas kernels: 87.9 us -> 85.7 us
    pallas_call x1, Pallas kernels: 87.9 us -> 85.7 us  [per_device(): pl.pallas_call(kernel, out_shape=(jax.ShapeDtypeStruct((2304, 128), F32),...]
where the time goes in v3:
time: 88.3 us; the launch traced here: 88.1 us
  Pallas kernels  85.7 us (97%)
  local copies, waits for them, and re-layouts  1.83 us (2%)
    pallas_call x1, Pallas kernels, per_device(): pl.pallas_call(kernel, out_shape=(jax.ShapeDtypeStruct((2304, 128), F32),...  85.7 us
    unnamed x2, local copies, waits for them, and re-layouts  1.83 us

profile of v3, /device:TPU:0, one launch (start us, length us, event | category | flops | bytes accessed | tf_op | source)
XLA Modules:
  0.0 88.1 jit_solution(3790156084676599616)
XLA Ops:
  0.6 85.7 %weight_grads.1 = (f32[2304,128]{1,0:T(8,128)S(1)}, f32[72,2048]{1,0:T(8,128)S(1)}) custom-call(bf16[128,2304]{1,0:T(8,128)(2,1)} %bitcast.7, bf16[256,2048]{1,0:T(8,128)(2,1)} %bitcast.6, bf16[128,2048]{1,0:T(8,128)(2,1)} %bitcast.9, bf16[256,1152]{1,0:T(8,128)(2,1)} %bitcast.8), custom_call_target="tpu_custom_call" | custom-call | tf_op jit(solution)/shard_map/weight_grads/pallas_call | solution.py:470
  86.3 1.0 %copy.8 = f32[2304,128]{1,0:T(8,128)} copy(f32[2304,128]{1,0:T(8,128)S(1)} %get-tuple-element.8) | data formatting | bytes 2359296
  87.3 0.8 copy.9

commit v4 on v3

--- a/solution.py
+++ b/solution.py
@@ -11,7 +11,7 @@
 
 (EXQ, EXO, GQ, GO, HQ, HO, OWNQ, OWNO, DQ, DO, RQ, RO, AQ, AO, PQ, PO, IQ, IO, LQ, LO, FQ, FO) = range(22)
 STEP = {1: 1, 2: -1, 3: 2}
-N_SEND, N_COME = 27, 96
+N_SEND, N_COME = 26, 96
 
 
 def kernel(
@@ -264,203 +264,215 @@
                 for copy, _ in copies[name]:
                     copy.wait_recv()
 
+    send((OWNQ, 0, 0), (OWNO, 0, 0))
+    send((EXO, 1, 0), (EXO, 2, 0))
     send((EXQ, 1, 0), (EXQ, 2, 0))
     send((GQ, 0, 1), (GQ, 0, -1))
+    left((EXO, 1, 0), (EXO, 2, 0))
     send((EXO, 3, 0))
     left((EXQ, 1, 0), (EXQ, 2, 0))
     send((EXQ, 3, 0))
+    left((GQ, 0, 1))
+    came((EXQ, 1, 0))
+    send((GQ, 1, 1), (GQ, 1, -1))
+    send((DQ, 0, 1), (DQ, 0, -1))
+    left((OWNO, 0, 0), (GQ, 0, -1))
+    left((EXO, 3, 0))
+    send((DO, 0, 1), (DO, 0, -1))
     came((EXQ, 2, 0))
     send((GQ, 2, 1), (GQ, 2, -1))
-    left((EXO, 3, 0))
-    send((DO, 0, 1), (DO, 0, -1))
-    left((GQ, 0, 1), (GQ, 0, -1))
-    left((EXQ, 3, 0))
-    send((DQ, 0, 1), (DQ, 0, -1))
-    send((EXO, 1, 0), (EXO, 2, 0))
-    came((EXQ, 1, 0))
-    send((GQ, 1, 1), (GQ, 1, -1))
-    left((GQ, 2, 1))
+    left((OWNQ, 0, 0))
+    left((GQ, 1, 1))
     came((EXQ, 3, 0))
     send((GQ, 3, 1), (GQ, 3, -1))
-    send((OWNQ, 0, 0), (OWNO, 0, 0))
     send((DQ, 1, 2))
+    left((EXQ, 3, 0))
     left((DQ, 0, -1))
     send((DQ, 1, -1))
+    came((GQ, 0, 1))
+    send((HQ, 0, 1))
+    left((GQ, 1, -1))
+    came((GQ, 2, 1), (GQ, 2, -1))
+    send((HQ, 2, 1), (HQ, 2, -1))
+    send((DQ, 1, 3))
+    send((GO, 0, 1), (GO, 0, -1))
+    left((DO, 0, 1), (DO, 0, -1))
+    send((DO, 1, 1), (DO, 1, -1))
+    left((GQ, 2, 1))
+    came((GQ, 1, -1))
+    send((HQ, 1, -1))
     left((GQ, 2, -1))
+    came((DQ, 1, 2))
+    send((RQ, 0, 0))
     came((DQ, 0, -1))
     send((RQ, 1, 0))
-    send((DQ, 1, 3))
-    came((GQ, 2, 1), (GQ, 2, -1))
-    send((HQ, 2, 1), (HQ, 2, -1))
-    left((EXO, 1, 0), (EXO, 2, 0), (GQ, 1, 1), (GQ, 1, -1))
-    came((GQ, 1, -1))
-    send((HQ, 1, -1))
+    came((DQ, 0, 1))
+    send((AQ, 0, 1), (AQ, 0, 2))
+    left((DQ, 0, 1), (GQ, 3, -1), (DQ, 1, 2))
+    came((DQ, 1, 3))
+    send((RQ, 0, 1), (AQ, 1, 1))
+    came((DO, 0, 1), (DO, 0, -1))
+    send((RO, 0, 1), (RO, 0, -1), (AO, 0, 0))
     came((EXO, 1, 0))
     send((GO, 1, 1), (GO, 1, -1))
-    came((GQ, 0, 1))
-    send((HQ, 0, 1))
-    left((OWNO, 0, 0))
-    left((DO, 0, 1), (DO, 0, -1))
-    send((DO, 1, 1), (DO, 1, -1))
-    came((DQ, 1, 2))
-    send((RQ, 0, 0))
-    came((DO, 0, 1), (DO, 0, -1))
-    send((RO, 0, 1), (RO, 0, -1), (AO, 0, 0))
-    left((DQ, 0, 1), (GQ, 3, -1), (OWNQ, 0, 0), (DQ, 1, 2))
-    came((DQ, 1, 3))
-    send((RQ, 0, 1), (AQ, 1, 1))
-    send((GO, 0, 1), (GO, 0, -1))
-    came((DQ, 0, 1))
-    send((AQ, 0, 1), (AQ, 0, 2))
+    left((DQ, 1, 3))
     came((GQ, 3, 1), (GQ, 3, -1))
     send((HQ, 3, 1), (HQ, 3, -1))
-    left((DQ, 1, 3), (HQ, 2, 1), (HQ, 2, -1))
-    came((DQ, 1, -1))
-    send((AQ, 1, 2))
+    left((GQ, 3, 1), (HQ, 2, -1), (DO, 1, 1), (DO, 1, -1), (AQ, 0, 1), (AQ, 0, 2))
     came((RQ, 0, 0))
     send((AQ, 0, 4))
+    came((DO, 1, 1), (DO, 1, -1))
+    send((RO, 1, 1), (RO, 1, -1), (AO, 1, 0))
+    left((HQ, 2, 1), (RQ, 0, 0), (AQ, 1, 1))
+    left((DQ, 1, -1), (RQ, 1, 0))
+    send((DQ, 2, -1))
     left((RQ, 0, 1))
     send((RQ, 3, 1))
-    left((RQ, 1, 0))
-    send((RQ, 2, 0))
-    left((GO, 1, -1), (AO, 0, 0), (AQ, 1, 1), (AQ, 0, 1), (AQ, 0, 2))
+    left((AO, 0, 0))
     came((RQ, 0, 1))
     send((AQ, 0, 5))
-    left((RQ, 0, 0))
-    send((DQ, 2, 1))
-    left((GQ, 3, 1))
     came((EXO, 2, 0))
     send((GO, 2, 1), (GO, 2, -1))
+    came((DQ, 1, -1))
+    send((RQ, 2, 0))
+    left((HQ, 0, 1), (GO, 0, 1), (GO, 0, -1), (HQ, 1, -1), (RO, 0, 1), (RO, 0, -1))
+    left((RQ, 3, 1))
+    send((DQ, 2, 1))
+    send((AQ, 1, 2))
     send((RQ, 3, 2))
+    came((RQ, 1, 0))
+    send((AQ, 1, 3))
     came((EXO, 3, 0))
     send((GO, 3, 1), (GO, 3, -1))
-    left((DQ, 1, -1))
-    send((DQ, 2, -1))
-    left((HQ, 1, -1), (HQ, 0, 1), (DO, 1, 1), (DO, 1, -1), (RO, 0, 1), (RO, 0, -1))
-    came((RQ, 1, 0))
-    send((AQ, 1, 3))
-    came((DO, 1, 1), (DO, 1, -1))
-    send((RO, 1, 1), (RO, 1, -1), (AO, 1, 0))
     came((GQ, 0, -1), (HQ, 0, 1), (GQ, 1, 1), (HQ, 1, -1), (HQ, 2, 1), (HQ, 2, -1), (HQ, 3, 1), (HQ, 3, -1))
     came((AQ, 0, 1), (AQ, 0, 2), (AQ, 0, 4), (AQ, 0, 5), (OWNQ, 0, 0))
     multiply_q(0)
     send((PQ, 0, 1), (PQ, 0, -1))
+    left((GO, 1, -1), (HQ, 3, 1), (HQ, 3, -1), (AQ, 0, 4), (RO, 1, 1), (RO, 1, -1), (AO, 1, 0), (AQ, 0, 5))
     came((AQ, 1, 1), (AQ, 1, 2), (AQ, 1, 3))
     multiply_q(1)
     send((PQ, 1, 1), (PQ, 1, -1))
-    came((GO, 1, -1))
-    send((HO, 1, -1))
-    left((GO, 0, 1), (GO, 0, -1), (HQ, 3, 1), (HQ, 3, -1), (AQ, 1, 2), (AQ, 0, 4))
-    came((RO, 1, 1), (RO, 1, -1))
-    send((AO, 3, 0))
     left((GO, 1, 1))
     came((GO, 0, 1))
     send((HO, 0, 1))
-    left((AQ, 0, 5), (AQ, 1, 3), (RO, 1, 1), (RO, 1, -1), (AO, 1, 0))
+    left((GO, 2, 1))
+    came((GO, 1, -1))
+    send((HO, 1, -1))
+    came((RO, 0, 1), (RO, 0, -1))
+    send((AO, 2, 0))
+    came((RO, 1, 1), (RO, 1, -1))
+    send((AO, 3, 0))
+    left((AQ, 1, 2), (AQ, 1, 3))
+    left((DQ, 2, -1))
+    send((DQ, 3, -1))
+    left((PQ, 0, 1))
+    send((IQ, 0, 1), (IQ, 0, -1))
+    send((IQ, 1, 1), (IQ, 1, -1))
     came((GO, 3, 1), (GO, 3, -1))
     send((HO, 3, 1), (HO, 3, -1))
-    left((PQ, 0, 1))
-    send((IQ, 0, 1), (IQ, 0, -1))
-    came((RO, 0, 1), (RO, 0, -1))
-    send((AO, 2, 0))
-    left((RQ, 3, 1), (GO, 2, 1), (GO, 2, -1), (RQ, 3, 2), (GO, 3, 1), (GO, 3, -1), (AO, 3, 0))
-    left((DQ, 2, -1))
-    send((DQ, 3, -1))
-    send((IQ, 1, 1), (IQ, 1, -1))
+    left((GO, 2, -1), (GO, 3, -1))
     left((DQ, 2, 1))
     send((DQ, 3, 1))
+    left((GO, 3, 1))
     came((GO, 2, 1), (GO, 2, -1))
     send((HO, 2, 1), (HO, 2, -1))
-    left((RQ, 2, 0), (PQ, 0, -1))
+    left((RQ, 3, 2), (PQ, 0, -1), (AO, 2, 0), (AO, 3, 0))
     came((OWNO, 0, 0), (AO, 0, 0), (AO, 1, 0), (AO, 2, 0), (AO, 3, 0), (GO, 0, -1), (HO, 0, 1), (GO, 1, 1))
     came((HO, 1, -1))
     multiply_o(True)
     came((DQ, 2, 1), (DQ, 2, -1), (RQ, 2, 0))
     send((AQ, 2, 0))
-    came((PQ, 0, 1), (PQ, 0, -1))
-    join_q(0)
-    send((LQ, 0, 1), (LQ, 0, -1))
-    left((PQ, 1, 1), (PQ, 1, -1), (HO, 1, -1), (HO, 0, 1), (HO, 3, 1), (HO, 3, -1), (AO, 2, 0), (HO, 2, 1))
-    left((HO, 2, -1))
+    left((RQ, 2, 0), (HO, 0, 1), (HO, 1, -1), (HO, 3, 1), (HO, 3, -1), (HO, 2, 1), (HO, 2, -1))
     came((HO, 2, 1), (HO, 2, -1), (HO, 3, 1), (HO, 3, -1))
     multiply_o(False)
-    send((PO, 2, 1), (PO, 2, -1))
-    send((PO, 3, 1), (PO, 3, -1))
-    send((IO, 3, 1), (IO, 3, -1))
     came((PQ, 1, 1), (PQ, 1, -1))
     join_q(1)
     send((LQ, 1, 1), (LQ, 1, -1))
-    came((DQ, 3, 1), (DQ, 3, -1), (RQ, 3, 1), (RQ, 3, 2))
-    send((AQ, 3, 0))
+    send((PO, 3, 1), (PO, 3, -1))
+    send((IO, 3, 1), (IO, 3, -1))
+    left((PQ, 1, 1), (PQ, 1, -1))
     came((AQ, 2, 0))
     multiply_q(2)
     send((PQ, 2, 1), (PQ, 2, -1))
     send((PO, 0, 1), (PO, 0, -1))
-    left((IQ, 0, 1), (IQ, 0, -1), (DQ, 3, -1), (IQ, 1, 1), (IQ, 1, -1), (DQ, 3, 1), (AQ, 2, 0))
-    left((PO, 2, 1))
-    send((IO, 2, 1), (IO, 2, -1))
+    came((DQ, 3, 1), (DQ, 3, -1), (RQ, 3, 1), (RQ, 3, 2))
+    send((AQ, 3, 0))
+    came((PQ, 0, 1), (PQ, 0, -1))
+    join_q(0)
+    send((LQ, 0, 1), (LQ, 0, -1))
+    send((PO, 2, 1), (PO, 2, -1))
+    left((DQ, 3, -1), (IQ, 0, 1), (IQ, 0, -1), (IQ, 1, 1), (IQ, 1, -1), (DQ, 3, 1), (AQ, 2, 0))
     came((PO, 3, 1), (PO, 3, -1))
     join_o(3)
     send((LO, 3, 1), (LO, 3, -1))
+    left((LQ, 1, 1), (LQ, 1, -1), (PO, 3, 1), (PO, 3, -1), (IO, 3, 1), (IO, 3, -1))
+    left((PO, 0, 1))
+    send((PO, 1, 1), (PO, 1, -1))
     came((AQ, 3, 0))
     multiply_q(3)
     send((PQ, 3, 1), (PQ, 3, -1))
-    send((IQ, 2, 1), (IQ, 2, -1))
-    left((PO, 0, 1))
-    send((PO, 1, 1), (PO, 1, -1))
-    left((LQ, 0, 1), (LQ, 0, -1), (PO, 2, -1), (PO, 3, 1), (PO, 3, -1), (IO, 3, 1), (IO, 3, -1), (AQ, 3, 0))
-    left((PO, 0, -1))
     came((IQ, 1, 1), (IQ, 1, -1), (LQ, 1, 1), (LQ, 1, -1))
     finish_q(1)
     send((FQ, 1, 0))
+    send((IQ, 2, 1), (IQ, 2, -1))
+    send((IO, 2, 1), (IO, 2, -1))
+    left((PO, 0, -1), (AQ, 3, 0), (PO, 2, 1), (PO, 2, -1))
+    came((IO, 3, 1), (IO, 3, -1), (LO, 3, 1), (LO, 3, -1))
+    finish_o(3)
     came((PO, 0, 1), (PO, 0, -1))
     join_o(0)
     send((LO, 0, 1), (LO, 0, -1))
-    came((PO, 2, 1), (PO, 2, -1))
-    join_o(2)
-    send((LO, 2, 1), (LO, 2, -1))
-    left((LQ, 1, 1), (LQ, 1, -1), (IO, 2, 1), (IO, 2, -1))
-    came((IO, 3, 1), (IO, 3, -1), (LO, 3, 1), (LO, 3, -1))
-    finish_o(3)
-    left((PQ, 2, 1), (PQ, 2, -1), (LO, 3, 1), (LO, 3, -1))
+    left((LO, 3, 1), (LO, 3, -1))
     came((PQ, 2, 1), (PQ, 2, -1))
     join_q(2)
     send((LQ, 2, 1), (LQ, 2, -1))
     send((IO, 0, 1), (IO, 0, -1))
+    send((IQ, 3, 1), (IQ, 3, -1))
+    left((PO, 1, 1))
     send((IO, 1, 1), (IO, 1, -1))
     came((PO, 1, 1), (PO, 1, -1))
     join_o(1)
     send((LO, 1, 1), (LO, 1, -1))
-    left((PO, 1, 1), (PO, 1, -1))
-    left((PQ, 3, 1))
-    send((IQ, 3, 1), (IQ, 3, -1))
+    left((PQ, 2, 1), (PQ, 2, -1), (LQ, 0, 1), (LQ, 0, -1), (PO, 1, -1))
+    came((PQ, 3, 1), (PQ, 3, -1))
+    join_q(3)
+    send((LQ, 3, 1), (LQ, 3, -1))
+    came((PO, 2, 1), (PO, 2, -1))
+    join_o(2)
+    send((LO, 2, 1), (LO, 2, -1))
+    left((PQ, 3, 1), (PQ, 3, -1), (IQ, 2, 1), (IQ, 2, -1), (IO, 2, 1), (IO, 2, -1), (LO, 0, 1), (LO, 0, -1))
+    left((IO, 0, 1), (IO, 0, -1), (IO, 1, -1))
+    came((IQ, 2, 1), (IQ, 2, -1), (LQ, 2, 1), (LQ, 2, -1))
+    finish_q(2)
+    send((FQ, 2, 0))
     came((IQ, 0, 1), (IQ, 0, -1), (LQ, 0, 1), (LQ, 0, -1))
     finish_q(0)
     send((FQ, 0, 0))
-    came((PQ, 3, 1), (PQ, 3, -1))
-    join_q(3)
-    send((LQ, 3, 1), (LQ, 3, -1))
-    left((PQ, 3, -1), (IQ, 2, 1), (IQ, 2, -1), (LO, 0, 1), (LO, 0, -1), (LO, 2, 1), (LO, 2, -1))
-    came((IQ, 2, 1), (IQ, 2, -1), (LQ, 2, 1), (LQ, 2, -1))
-    finish_q(2)
-    send((FQ, 2, 0))
-    left((LQ, 2, 1), (LQ, 2, -1), (IO, 0, 1), (IO, 0, -1), (IO, 1, 1), (IO, 1, -1))
+    came((IO, 0, 1), (IO, 0, -1), (LO, 0, 1), (LO, 0, -1))
+    finish_o(0)
+    send((FO, 0, 0))
+    left((LQ, 2, 1), (LQ, 2, -1), (IQ, 3, 1), (IQ, 3, -1), (IO, 1, 1), (LO, 1, 1), (LO, 1, -1))
+    came((IO, 2, 1), (IO, 2, -1), (LO, 2, 1), (LO, 2, -1))
+    finish_o(2)
+    send((FO, 2, 0))
+    left((LQ, 3, -1), (LO, 2, 1), (LO, 2, -1))
+    came((IQ, 3, 1), (IQ, 3, -1), (LQ, 3, 1), (LQ, 3, -1))
+    finish_q(3)
     came((IO, 1, 1), (IO, 1, -1), (LO, 1, 1), (LO, 1, -1))
     finish_o(1)
     send((FO, 1, 0))
-    came((IO, 0, 1), (IO, 0, -1), (LO, 0, 1), (LO, 0, -1))
-    finish_o(0)
-    send((FO, 0, 0))
-    came((IO, 2, 1), (IO, 2, -1), (LO, 2, 1), (LO, 2, -1))
-    finish_o(2)
-    send((FO, 2, 0))
-    left((LO, 1, 1), (LO, 1, -1))
-    came((IQ, 3, 1), (IQ, 3, -1), (LQ, 3, 1), (LQ, 3, -1))
-    finish_q(3)
 
     came(*list(open_came))
     left(*list(open_left))
     assert len(arrivals) == N_COME and len(locals_) == 7, len(arrivals)
+
+
+def store(q_ref, o_ref, out_q, out_o, sem):
+    copies = [pltpu.make_async_copy(q_ref, out_q, sem.at[0]), pltpu.make_async_copy(o_ref, out_o, sem.at[1])]
+    for copy in copies:
+        copy.start()
+    for copy in copies:
+        copy.wait()
 
 
 def per_device(normed, qkv_grad, attn_out, out_grad):
@@ -501,6 +513,18 @@
         ),
         name="weight_grads",
     )(*[pltpu.with_memory_space_constraint(v, pltpu.HBM) for v in flat])
+    out_q, out_o = pl.pallas_call(
+        store,
+        out_shape=(
+            jax.ShapeDtypeStruct((2304, 128), F32),
+            jax.ShapeDtypeStruct((72, 2048), F32),
+        ),
+        in_specs=[vmem] * 2,
+        out_specs=[hbm] * 2,
+        scratch_shapes=[pltpu.SemaphoreType.DMA((2,))],
+        compiler_params=pltpu.CompilerParams(vmem_limit_bytes=1024 * 1024),
+        name="store",
+    )(out_q, out_o)
     return out_q, out_o.T
 
 

time: 88.3 us -> 87.6 us (level)
  local copies, waits for them, and re-layouts: 1.83 us -> 0 us
  Pallas kernels: 85.7 us -> 86.7 us
    unnamed x2 -> x0, local copies, waits for them, and re-layouts: 1.83 us -> none
    pallas_call x0 -> x1, Pallas kernels: none -> 1.22 us  [per_device(): pl.pallas_call(store, out_shape=(jax.ShapeDtypeStruct((2304, 128), F32),...]
where the time goes in v4:
time: 87.6 us; the launch traced here: 87.4 us
  Pallas kernels  86.7 us (99%)
    pallas_call x1, Pallas kernels, per_device(): pl.pallas_call(kernel, out_shape=(jax.ShapeDtypeStruct((2304, 128), F32),...  85.5 us

profile of v4, /device:TPU:0, one launch (start us, length us, event | category | flops | bytes accessed | tf_op | source)
XLA Modules:
  0.0 87.4 jit_solution(2351640999271349921)
XLA Ops:
  0.6 85.5 %weight_grads.1 = (f32[2304,128]{1,0:T(8,128)S(1)}, f32[72,2048]{1,0:T(8,128)S(1)}) custom-call(bf16[128,2304]{1,0:T(8,128)(2,1)} %bitcast.6, bf16[256,2048]{1,0:T(8,128)(2,1)} %bitcast.5, bf16[128,2048]{1,0:T(8,128)(2,1)} %bitcast.8, bf16[256,1152]{1,0:T(8,128)(2,1)} %bitcast.7), custom_call_target="tpu_custom_call" | custom-call | tf_op jit(solution)/shard_map/weight_grads/pallas_call | solution.py:482
  86.1 1.2 %store.1 = (f32[2304,128]{1,0:T(8,128)}, f32[72,2048]{1,0:T(8,128)}) custom-call(f32[2304,128]{1,0:T(8,128)S(1)} %get-tuple-element.6.q_ref, f32[72,2048]{1,0:T(8,128)S(1)} %get-tuple-element.7.o_ref), custom_call_target="tpu_custom_call" | custom-call | tf_op jit(solution)/shard_map/store/pallas_call | solution.py:516

commit v5 on v4

--- a/solution.py
+++ b/solution.py
@@ -11,7 +11,7 @@
 
 (EXQ, EXO, GQ, GO, HQ, HO, OWNQ, OWNO, DQ, DO, RQ, RO, AQ, AO, PQ, PO, IQ, IO, LQ, LO, FQ, FO) = range(22)
 STEP = {1: 1, 2: -1, 3: 2}
-N_SEND, N_COME = 26, 96
+N_SEND, N_COME = 24, 69
 
 
 def kernel(
@@ -222,6 +222,26 @@
                 whole[i, s, step] = whole[l, s, step] = rest
     for p in (2, 3):
         whole[AQ, p, 0] = vb_q.at[1:4, mine, lanes(order_q[p] * 512, 512)]
+    together = at_q.at[:, 0:768]
+    for name in ((GQ, 0, -1), (HQ, 0, 1), (GQ, 1, 1), (HQ, 1, -1), (HQ, 2, 1), (HQ, 2, -1), (HQ, 3, 1), (HQ, 3, -1)):
+        whole[name] = together
+    together = va_o.at[0]
+    for name in ((GO, 0, -1), (HO, 0, 1), (GO, 1, 1), (HO, 1, -1)):
+        whole[name] = together
+    together = va_o.at[2, 0:2]
+    for name in ((HO, 2, 1), (HO, 2, -1), (HO, 3, 1), (HO, 3, -1)):
+        whole[name] = together
+    together = bt_o.at[:, :, 0:1024]
+    for name in ((OWNO, 0, 0), (AO, 0, 0), (AO, 1, 0), (AO, 2, 0), (AO, 3, 0)):
+        whole[name] = together
+    for p in (0, 1):
+        two = bt_o.at[2 * p:2 * p + 2, :, 0:512]
+        one = bt_o.at[2 * p:2 * p + 2, :, 0:256]
+        for step in (1, -1):
+            whole[DO, p, step], whole[RO, p, step] = two, one
+    three_q, three_o = out_q.at[0:1728], out_o.at[:, 0:1536]
+    for s in range(3):
+        whole[FQ, s, 0], whole[FO, s, 0] = three_q, three_o
     copies, arrivals, free = {}, {}, list(range(N_SEND))
     open_left, open_came = {}, {}
 
@@ -258,7 +278,7 @@
                 ).wait_recv()
                 for other in whole:
                     if whole[other] is both:
-                        del open_came[other]
+                        open_came.pop(other, None)
             else:
                 del open_came[name]
                 for copy, _ in copies[name]:
@@ -298,12 +318,12 @@
     send((GO, 0, 1), (GO, 0, -1))
     left((DO, 0, 1), (DO, 0, -1))
     send((DO, 1, 1), (DO, 1, -1))
+    left((GQ, 2, -1))
+    came((DQ, 1, 2))
+    send((RQ, 0, 0))
     left((GQ, 2, 1))
     came((GQ, 1, -1))
     send((HQ, 1, -1))
-    left((GQ, 2, -1))
-    came((DQ, 1, 2))
-    send((RQ, 0, 0))
     came((DQ, 0, -1))
     send((RQ, 1, 0))
     came((DQ, 0, 1))
@@ -315,15 +335,15 @@
     send((RO, 0, 1), (RO, 0, -1), (AO, 0, 0))
     came((EXO, 1, 0))
     send((GO, 1, 1), (GO, 1, -1))
-    left((DQ, 1, 3))
+    left((HQ, 2, -1), (DQ, 1, 3))
     came((GQ, 3, 1), (GQ, 3, -1))
     send((HQ, 3, 1), (HQ, 3, -1))
-    left((GQ, 3, 1), (HQ, 2, -1), (DO, 1, 1), (DO, 1, -1), (AQ, 0, 1), (AQ, 0, 2))
+    left((GQ, 3, 1), (DO, 1, 1), (DO, 1, -1), (AQ, 0, 1), (AQ, 0, 2))
     came((RQ, 0, 0))
     send((AQ, 0, 4))
     came((DO, 1, 1), (DO, 1, -1))
     send((RO, 1, 1), (RO, 1, -1), (AO, 1, 0))
-    left((HQ, 2, 1), (RQ, 0, 0), (AQ, 1, 1))
+    left((HQ, 2, 1), (GO, 0, -1), (RQ, 0, 0), (AQ, 1, 1))
     left((DQ, 1, -1), (RQ, 1, 0))
     send((DQ, 2, -1))
     left((RQ, 0, 1))
@@ -335,20 +355,21 @@
     send((GO, 2, 1), (GO, 2, -1))
     came((DQ, 1, -1))
     send((RQ, 2, 0))
-    left((HQ, 0, 1), (GO, 0, 1), (GO, 0, -1), (HQ, 1, -1), (RO, 0, 1), (RO, 0, -1))
+    left((HQ, 0, 1), (GO, 0, 1), (RO, 0, 1), (RO, 0, -1))
     left((RQ, 3, 1))
     send((DQ, 2, 1))
+    send((RQ, 3, 2))
     send((AQ, 1, 2))
-    send((RQ, 3, 2))
     came((RQ, 1, 0))
     send((AQ, 1, 3))
     came((EXO, 3, 0))
     send((GO, 3, 1), (GO, 3, -1))
+    left((HQ, 1, -1), (HQ, 3, 1), (HQ, 3, -1), (AQ, 0, 4), (AO, 1, 0), (AQ, 0, 5))
     came((GQ, 0, -1), (HQ, 0, 1), (GQ, 1, 1), (HQ, 1, -1), (HQ, 2, 1), (HQ, 2, -1), (HQ, 3, 1), (HQ, 3, -1))
     came((AQ, 0, 1), (AQ, 0, 2), (AQ, 0, 4), (AQ, 0, 5), (OWNQ, 0, 0))
     multiply_q(0)
     send((PQ, 0, 1), (PQ, 0, -1))
-    left((GO, 1, -1), (HQ, 3, 1), (HQ, 3, -1), (AQ, 0, 4), (RO, 1, 1), (RO, 1, -1), (AO, 1, 0), (AQ, 0, 5))
+    left((GO, 1, -1), (RO, 1, 1), (RO, 1, -1))
     came((AQ, 1, 1), (AQ, 1, 2), (AQ, 1, 3))
     multiply_q(1)
     send((PQ, 1, 1), (PQ, 1, -1))
@@ -363,14 +384,13 @@
     came((RO, 1, 1), (RO, 1, -1))
     send((AO, 3, 0))
     left((AQ, 1, 2), (AQ, 1, 3))
+    left((PQ, 0, 1))
+    send((IQ, 0, 1), (IQ, 0, -1))
+    left((GO, 2, -1), (GO, 3, -1))
     left((DQ, 2, -1))
     send((DQ, 3, -1))
-    left((PQ, 0, 1))
-    send((IQ, 0, 1), (IQ, 0, -1))
-    send((IQ, 1, 1), (IQ, 1, -1))
     came((GO, 3, 1), (GO, 3, -1))
     send((HO, 3, 1), (HO, 3, -1))
-    left((GO, 2, -1), (GO, 3, -1))
     left((DQ, 2, 1))
     send((DQ, 3, 1))
     left((GO, 3, 1))
@@ -382,7 +402,7 @@
     multiply_o(True)
     came((DQ, 2, 1), (DQ, 2, -1), (RQ, 2, 0))
     send((AQ, 2, 0))
-    left((RQ, 2, 0), (HO, 0, 1), (HO, 1, -1), (HO, 3, 1), (HO, 3, -1), (HO, 2, 1), (HO, 2, -1))
+    send((IQ, 1, 1), (IQ, 1, -1))
     came((HO, 2, 1), (HO, 2, -1), (HO, 3, 1), (HO, 3, -1))
     multiply_o(False)
     came((PQ, 1, 1), (PQ, 1, -1))
@@ -390,7 +410,8 @@
     send((LQ, 1, 1), (LQ, 1, -1))
     send((PO, 3, 1), (PO, 3, -1))
     send((IO, 3, 1), (IO, 3, -1))
-    left((PQ, 1, 1), (PQ, 1, -1))
+    left((RQ, 2, 0), (PQ, 1, 1), (PQ, 1, -1), (HO, 0, 1), (HO, 1, -1), (IQ, 0, 1), (IQ, 0, -1), (HO, 3, 1))
+    left((HO, 3, -1), (HO, 2, 1), (HO, 2, -1))
     came((AQ, 2, 0))
     multiply_q(2)
     send((PQ, 2, 1), (PQ, 2, -1))
@@ -401,22 +422,22 @@
     join_q(0)
     send((LQ, 0, 1), (LQ, 0, -1))
     send((PO, 2, 1), (PO, 2, -1))
-    left((DQ, 3, -1), (IQ, 0, 1), (IQ, 0, -1), (IQ, 1, 1), (IQ, 1, -1), (DQ, 3, 1), (AQ, 2, 0))
+    left((DQ, 3, -1), (DQ, 3, 1), (AQ, 2, 0), (IQ, 1, 1), (IQ, 1, -1))
     came((PO, 3, 1), (PO, 3, -1))
     join_o(3)
     send((LO, 3, 1), (LO, 3, -1))
-    left((LQ, 1, 1), (LQ, 1, -1), (PO, 3, 1), (PO, 3, -1), (IO, 3, 1), (IO, 3, -1))
-    left((PO, 0, 1))
-    send((PO, 1, 1), (PO, 1, -1))
+    left((PO, 3, 1), (PO, 3, -1), (IO, 3, 1), (IO, 3, -1))
     came((AQ, 3, 0))
     multiply_q(3)
     send((PQ, 3, 1), (PQ, 3, -1))
+    left((PO, 0, 1))
+    send((PO, 1, 1), (PO, 1, -1))
     came((IQ, 1, 1), (IQ, 1, -1), (LQ, 1, 1), (LQ, 1, -1))
     finish_q(1)
     send((FQ, 1, 0))
     send((IQ, 2, 1), (IQ, 2, -1))
     send((IO, 2, 1), (IO, 2, -1))
-    left((PO, 0, -1), (AQ, 3, 0), (PO, 2, 1), (PO, 2, -1))
+    left((LQ, 1, 1), (LQ, 1, -1), (PO, 0, -1), (AQ, 3, 0), (PO, 2, 1), (PO, 2, -1))
     came((IO, 3, 1), (IO, 3, -1), (LO, 3, 1), (LO, 3, -1))
     finish_o(3)
     came((PO, 0, 1), (PO, 0, -1))
@@ -428,20 +449,20 @@
     send((LQ, 2, 1), (LQ, 2, -1))
     send((IO, 0, 1), (IO, 0, -1))
     send((IQ, 3, 1), (IQ, 3, -1))
+    left((PQ, 2, 1), (PQ, 2, -1), (LQ, 0, 1), (LQ, 0, -1))
     left((PO, 1, 1))
     send((IO, 1, 1), (IO, 1, -1))
     came((PO, 1, 1), (PO, 1, -1))
     join_o(1)
     send((LO, 1, 1), (LO, 1, -1))
-    left((PQ, 2, 1), (PQ, 2, -1), (LQ, 0, 1), (LQ, 0, -1), (PO, 1, -1))
+    left((PO, 1, -1), (IO, 2, 1), (IO, 2, -1))
     came((PQ, 3, 1), (PQ, 3, -1))
     join_q(3)
     send((LQ, 3, 1), (LQ, 3, -1))
     came((PO, 2, 1), (PO, 2, -1))
     join_o(2)
     send((LO, 2, 1), (LO, 2, -1))
-    left((PQ, 3, 1), (PQ, 3, -1), (IQ, 2, 1), (IQ, 2, -1), (IO, 2, 1), (IO, 2, -1), (LO, 0, 1), (LO, 0, -1))
-    left((IO, 0, 1), (IO, 0, -1), (IO, 1, -1))
+    left((PQ, 3, 1), (PQ, 3, -1), (IQ, 2, 1), (IQ, 2, -1), (LO, 0, 1), (LO, 0, -1))
     came((IQ, 2, 1), (IQ, 2, -1), (LQ, 2, 1), (LQ, 2, -1))
     finish_q(2)
     send((FQ, 2, 0))
@@ -451,11 +472,11 @@
     came((IO, 0, 1), (IO, 0, -1), (LO, 0, 1), (LO, 0, -1))
     finish_o(0)
     send((FO, 0, 0))
-    left((LQ, 2, 1), (LQ, 2, -1), (IQ, 3, 1), (IQ, 3, -1), (IO, 1, 1), (LO, 1, 1), (LO, 1, -1))
+    left((LQ, 2, 1), (LQ, 2, -1), (IO, 0, 1), (IO, 0, -1), (IQ, 3, 1), (IQ, 3, -1), (IO, 1, 1), (IO, 1, -1))
+    left((LO, 1, 1), (LO, 1, -1), (LO, 2, 1), (LO, 2, -1))
     came((IO, 2, 1), (IO, 2, -1), (LO, 2, 1), (LO, 2, -1))
     finish_o(2)
     send((FO, 2, 0))
-    left((LQ, 3, -1), (LO, 2, 1), (LO, 2, -1))
     came((IQ, 3, 1), (IQ, 3, -1), (LQ, 3, 1), (LQ, 3, -1))
     finish_q(3)
     came((IO, 1, 1), (IO, 1, -1), (LO, 1, 1), (LO, 1, -1))

time: 87.6 us -> 87.2 us (level)
  no operation moved by 1% of the time
where the time goes in v5:
time: 87.2 us; the launch traced here: 87.1 us
  Pallas kernels  86.5 us (99%)
    pallas_call x1, Pallas kernels, per_device(): pl.pallas_call(kernel, out_shape=(jax.ShapeDtypeStruct((2304, 128), F32),...  85.2 us

profile of v5, /device:TPU:0, one launch (start us, length us, event | category | flops | bytes accessed | tf_op | source)
XLA Modules:
  0.0 87.1 jit_solution(1393504344707004512)
XLA Ops:
  0.6 85.2 %weight_grads.1 = (f32[2304,128]{1,0:T(8,128)S(1)}, f32[72,2048]{1,0:T(8,128)S(1)}) custom-call(bf16[128,2304]{1,0:T(8,128)(2,1)} %bitcast.6, bf16[256,2048]{1,0:T(8,128)(2,1)} %bitcast.5, bf16[128,2048]{1,0:T(8,128)(2,1)} %bitcast.8, bf16[256,1152]{1,0:T(8,128)(2,1)} %bitcast.7), custom_call_target="tpu_custom_call" | custom-call | tf_op jit(solution)/shard_map/weight_grads/pallas_call | solution.py:503
  85.9 1.2 %store.1 = (f32[2304,128]{1,0:T(8,128)}, f32[72,2048]{1,0:T(8,128)}) custom-call(f32[2304,128]{1,0:T(8,128)S(1)} %get-tuple-element.6.q_ref, f32[72,2048]{1,0:T(8,128)S(1)} %get-tuple-element.7.o_ref), custom_call_target="tpu_custom_call" | custom-call | tf_op jit(solution)/shard_map/store/pallas_call | solution.py:537

commit v6 on v5

--- a/solution.py
+++ b/solution.py
@@ -63,9 +63,6 @@
 
     load_la_q.wait()
     ta_q[...] = la_q[...].T
-    at_q[:, lanes(x * 128)] = ta_q[features(z), :]
-    load_lb_o.wait()
-    bt_o[:, :, lanes(row * 256, 256)] = lb_o[...].T.reshape(4, 288, 256)
     for copy in loads:
         copy.wait()
     pl.semaphore_wait(barrier, len(peers))
@@ -284,10 +281,13 @@
                 for copy, _ in copies[name]:
                     copy.wait_recv()
 
-    send((OWNQ, 0, 0), (OWNO, 0, 0))
-    send((EXO, 1, 0), (EXO, 2, 0))
     send((EXQ, 1, 0), (EXQ, 2, 0))
     send((GQ, 0, 1), (GQ, 0, -1))
+    send((EXO, 1, 0), (EXO, 2, 0), (OWNQ, 0, 0))
+    at_q[:, lanes(x * 128)] = ta_q[features(z), :]
+    load_lb_o.wait()
+    bt_o[:, :, lanes(row * 256, 256)] = lb_o[...].T.reshape(4, 288, 256)
+    send((OWNO, 0, 0))
     left((EXO, 1, 0), (EXO, 2, 0))
     send((EXO, 3, 0))
     left((EXQ, 1, 0), (EXQ, 2, 0))

time: 87.2 us -> 87.2 us (level)
  no operation moved by 1% of the time
where the time goes in v6:
time: 87.2 us; the launch traced here: 87.1 us
  Pallas kernels  86.5 us (99%)
    pallas_call x1, Pallas kernels, per_device(): pl.pallas_call(kernel, out_shape=(jax.ShapeDtypeStruct((2304, 128), F32),...  85.2 us

profile of v6, /device:TPU:0, one launch (start us, length us, event | category | flops | bytes accessed | tf_op | source)
XLA Modules:
  0.0 87.1 jit_solution(5948602122034986407)
XLA Ops:
  0.6 85.2 %weight_grads.1 = (f32[2304,128]{1,0:T(8,128)S(1)}, f32[72,2048]{1,0:T(8,128)S(1)}) custom-call(bf16[128,2304]{1,0:T(8,128)(2,1)} %bitcast.6, bf16[256,2048]{1,0:T(8,128)(2,1)} %bitcast.5, bf16[128,2048]{1,0:T(8,128)(2,1)} %bitcast.8, bf16[256,1152]{1,0:T(8,128)(2,1)} %bitcast.7), custom_call_target="tpu_custom_call" | custom-call | tf_op jit(solution)/shard_map/weight_grads/pallas_call | solution.py:503
  85.9 1.2 %store.1 = (f32[2304,128]{1,0:T(8,128)}, f32[72,2048]{1,0:T(8,128)}) custom-call(f32[2304,128]{1,0:T(8,128)S(1)} %get-tuple-element.6.q_ref, f32[72,2048]{1,0:T(8,128)S(1)} %get-tuple-element.7.o_ref), custom_call_target="tpu_custom_call" | custom-call | tf_op jit(solution)/shard_map/store/pallas_call | solution.py:537

commit v7 on v6

--- a/solution.py
+++ b/solution.py
@@ -489,7 +489,10 @@
 
 
 def store(q_ref, o_ref, out_q, out_o, sem):
-    copies = [pltpu.make_async_copy(q_ref, out_q, sem.at[0]), pltpu.make_async_copy(o_ref, out_o, sem.at[1])]
+    copies = [pltpu.make_async_copy(o_ref, out_o, sem.at[4])]
+    for k in range(4):
+        rows = pl.ds(k * 576, 576)
+        copies.append(pltpu.make_async_copy(q_ref.at[rows], out_q.at[rows], sem.at[k]))
     for copy in copies:
         copy.start()
     for copy in copies:
@@ -542,7 +545,7 @@
         ),
         in_specs=[vmem] * 2,
         out_specs=[hbm] * 2,
-        scratch_shapes=[pltpu.SemaphoreType.DMA((2,))],
+        scratch_shapes=[pltpu.SemaphoreType.DMA((5,))],
         compiler_params=pltpu.CompilerParams(vmem_limit_bytes=1024 * 1024),
         name="store",
     )(out_q, out_o)

time: 87.2 us -> 87.3 us (level)
  no operation moved by 1% of the time
where the time goes in v7:
time: 87.3 us; the launch traced here: 87.1 us
  Pallas kernels  86.5 us (99%)
    pallas_call x1, Pallas kernels, per_device(): pl.pallas_call(kernel, out_shape=(jax.ShapeDtypeStruct((2304, 128), F32),...  85.2 us

profile of v7, /device:TPU:0, one launch (start us, length us, event | category | flops | bytes accessed | tf_op | source)
XLA Modules:
  0.0 87.1 jit_solution(18135514035087953466)
XLA Ops:
  0.6 85.2 %weight_grads.1 = (f32[2304,128]{1,0:T(8,128)S(1)}, f32[72,2048]{1,0:T(8,128)S(1)}) custom-call(bf16[128,2304]{1,0:T(8,128)(2,1)} %bitcast.6, bf16[256,2048]{1,0:T(8,128)(2,1)} %bitcast.5, bf16[128,2048]{1,0:T(8,128)(2,1)} %bitcast.8, bf16[256,1152]{1,0:T(8,128)(2,1)} %bitcast.7), custom_call_target="tpu_custom_call" | custom-call | tf_op jit(solution)/shard_map/weight_grads/pallas_call | solution.py:506
  85.9 1.2 %store.1 = (f32[2304,128]{1,0:T(8,128)}, f32[72,2048]{1,0:T(8,128)}) custom-call(f32[2304,128]{1,0:T(8,128)S(1)} %get-tuple-element.6.q_ref, f32[72,2048]{1,0:T(8,128)S(1)} %get-tuple-element.7.o_ref), custom_call_target="tpu_custom_call" | custom-call | tf_op jit(solution)/shard_map/store/pallas_call | solution.py:540
